TPU v7x, 32 devices: a whole 2x2x4 slice. The times are simulated.
32 devices in a mesh: fsdp: 4 (over z), seq: 8 (over y, x, core).
Axes of the slice: x: 2, y: 2, z: 4, core: 2. Of those that a mesh axis runs over, the one named last changes fastest.
Arguments:
- timestep: int32 [4], P('fsdp'), may hold values from 0 to 999
- pooled: bfloat16 [4, 3072], P('fsdp'), may hold values from -6 to 6
- modulation_weight: bfloat16 [3072, 9216], P('fsdp', 'seq'), may hold values from -0.109375 to 0.109375
- reference_attention: bfloat16 [4, 2, 512, 1536], P('fsdp', None, 'seq'), may hold values from -6 to 6
- policy_attention: bfloat16 [4, 2, 512, 1536], P('fsdp', None, 'seq'), may hold values from -6 to 6
- reference_residual: bfloat16 [4, 2, 512, 3072], P('fsdp', None, 'seq'), may hold values from -6 to 6
- policy_residual: bfloat16 [4, 2, 512, 3072], P('fsdp', None, 'seq'), may hold values from -6 to 6
- noise: float32 [4, 2, 512, 64], P('fsdp', None, 'seq'), may hold values from -6 to 6
- latent: float32 [4, 2, 512, 64], P('fsdp', None, 'seq'), may hold values from -3 to 3
- frozen_output_weight: bfloat16 [1536, 3072], P(None, 'fsdp'), may hold values from -0.15625 to 0.15625
- adapter_down_weight: bfloat16 [64, 1536], P(None, 'fsdp'), may hold values from -0.15625 to 0.15625
- adapter_up_weight: bfloat16 [64, 3072], P(None, 'fsdp'), may hold values from -0.75 to 0.75
- reference_head: bfloat16 [64, 3072], P(None, 'fsdp'), may hold values from -0.109375 to 0.109375
- policy_head: bfloat16 [64, 3072], P(None, 'fsdp'), may hold values from -0.109375 to 0.109375
Outputs:
- loss: float32 [4], P('fsdp')
- grad_down: float32 [64, 1536], P(None, 'fsdp')
- grad_up: float32 [64, 3072], P(None, 'fsdp')
- grad_head: float32 [64, 3072], P(None, 'fsdp')
- grad_resid: bfloat16 [4, 2, 512, 3072], P('fsdp', None, 'seq')
- grad_attn: bfloat16 [4, 2, 512, 1536], P('fsdp', None, 'seq')
All inputs are finite; a program needn't handle non-finite values.
Results may differ from a plain program's by a relative error of at most 0.029.
Values may be sent and summed in bfloat16 or wider, within the bound.
No kernel may reach another device: no remote copies, remote signals or barrier semaphores. Data moves between devices by JAX's collectives and lax.ppermute only.
A program may use at most 64 MiB of HBM per device.

v0:
```python
import math

import jax
import jax.numpy as jnp
from jax import lax
from jax.experimental import pallas as pl
from jax.experimental.pallas import tpu as pltpu
from jax.sharding import PartitionSpec as P


EPSILON = 1e-06


def embedding(timestep, layer_width):
    half_width = layer_width // 2
    frequency = jnp.exp(-math.log(10000.0) * jnp.arange(half_width, dtype=jnp.float32) / half_width)
    angles = timestep.astype(jnp.float32)[:, None] * frequency[None, :]
    return jnp.concatenate([jnp.cos(angles), jnp.sin(angles)], axis=1)


def contract_rows(left, right):
    return lax.dot_general(
        left, right, (((0,), (0,)), ((), ())), preferred_element_type=jnp.float32
    )


def contracted_columns(left, right):
    return lax.dot_general(
        left, right, (((1,), (1,)), ((), ())), preferred_element_type=jnp.float32
    )


def shift(value, step):
    count = lax.axis_size("fsdp")
    return lax.ppermute(value, "fsdp", [(i, (i + step) % count) for i in range(count)])


def swap(value, mask):
    count = lax.axis_size("seq")
    return lax.ppermute(value, "seq", [(i, i ^ mask) for i in range(count)])


def pick(value, index, axis=0):
    return lax.dynamic_index_in_dim(value, index, axis, keepdims=False)


def in_order(pieces, index):
    stacked = jnp.stack(pieces)
    places = [pick(stacked, index ^ place) for place in range(len(pieces))]
    return jnp.stack(places)


def gather_seq(value, seq_index):
    count = lax.axis_size("seq")
    plane = [value] + [swap(value, 2 * mask) for mask in range(1, count // 2)]
    stacked = jnp.stack(plane)
    other = swap(stacked, 1)
    both = []
    for mask in range(count // 2):
        both += [stacked[mask], other[mask]]
    return in_order(both, seq_index)


def final_layer(projected, residual, gate_row, shift_row, scale_row, head):
    stream = residual.astype(jnp.float32) + gate_row * projected
    row_mean = jnp.mean(stream, axis=1, keepdims=True)
    centred = stream - row_mean
    variance = jnp.mean(centred * centred, axis=1, keepdims=True)
    inv_std = lax.rsqrt(variance + EPSILON)
    normed = centred * inv_std
    modulated = (normed * (1.0 + scale_row) + shift_row).astype(jnp.bfloat16)
    predicted = contracted_columns(modulated, head)
    return (normed, inv_std, modulated, predicted)


def member_errors(predicted, target, scale_total):
    offset = predicted - target
    squared = jnp.sum(offset * offset, axis=1)
    return jnp.sum(squared.reshape(2, -1), axis=1) / scale_total


def gather_weights(ext, fsdp_index, seq_index):
    rows, columns = ext.shape
    count_f, count_s = lax.axis_size("fsdp"), lax.axis_size("seq")
    part = rows // count_s
    chunk = lax.dynamic_slice(ext, (seq_index * part, 0), (part, columns))
    full = jnp.zeros((rows, columns * count_f), ext.dtype)
    full = lax.dynamic_update_slice(full, ext, (0, fsdp_index * columns))
    arrived = [shift(chunk, step) for step in range(1, count_f)]
    group = -(-len(arrived) // 3)
    for first in range(1, count_f, group):
        steps = range(first, min(first + group, count_f))
        own = jnp.concatenate([arrived[step - 1] for step in steps], axis=0)
        plane = [own] + [swap(own, 2 * mask) for mask in range(1, count_s // 2)]
        pieces = []
        for piece in plane:
            pieces += [piece, swap(piece, 1)]

        def place(at, full, piece, mask):
            row = (seq_index ^ mask) * part
            column = ((fsdp_index - first - at) % count_f) * columns
            held = lax.dynamic_slice(piece, (at * part, 0), (part, columns))
            return lax.dynamic_update_slice(full, held, (row, column))

        for mask, piece in enumerate(pieces):
            if group == 1:
                full = place(0, full, piece, mask)
            else:
                full = lax.fori_loop(
                    0, len(steps), lambda at, held: place(at, held, piece, mask), full
                )
    return full


def dot(left, right):
    return jnp.dot(left, right, preferred_element_type=jnp.float32)


def margin_lanes(filled, seq_index, rounded):
    lane = lax.broadcasted_iota(jnp.int32, filled.shape, 1) - 3 * seq_index
    high = rounded(filled)
    middle = rounded(filled - high)
    low = filled - high - middle
    return jnp.where(
        lane == 0, high, jnp.where(lane == 1, middle, jnp.where(lane == 2, low, 0.0))
    )


def step_kernel(sizes, where, *refs):
    tokens, features, width, rank, channels, count_f, count_s, scale_total, spans = sizes
    block, down_block = width // count_f, features // count_f
    part, small_part = features // count_s, (2 * rank + 2 * channels) // count_s
    (attn_pol, attn_ref, res_pol, res_ref, noise, latent, own, own_small), refs = refs[:8], refs[8:]
    mod_pieces, refs = refs[:count_s], refs[count_s:]
    chunks, refs = refs[: len(spans)], refs[len(spans) :]
    keep, send, dstream_out, attn_out, refs = *refs[:4], refs[4:]
    rows, base, small, residual, proj, z_hold, back, dproj, mod_hold, mod, sems = refs
    fsdp_index, seq_index = where[0], where[1]

    def start(source, target, slot):
        copy = pltpu.make_async_copy(source, target, sems.at[slot])
        copy.start()
        return copy

    first = [
        start(attn_pol, rows.at[:tokens], 0),
        start(attn_ref, rows.at[tokens:], 1),
    ]
    blocks = [[start(own, base.at[fsdp_index], 2)]] + [[] for _ in range(1, count_f)]
    smalls = [start(own_small, small.at[fsdp_index], 3)]
    slot = 6
    for chunk, (step, mask, first_row, count) in zip(chunks, spans):
        at = lax.rem(fsdp_index - step + count_f, count_f)
        place = lax.bitwise_xor(seq_index, mask)
        wide = max(0, min(part - first_row, count))
        if wide:
            row = pl.multiple_of(place * part + first_row, 16)
            blocks[step].append(
                start(chunk.at[:wide], base.at[at, pl.ds(row, wide)], slot)
            )
        if wide < count:
            row = pl.multiple_of(place * small_part + (first_row + wide - part), 16)
            smalls.append(
                start(chunk.at[wide:], small.at[at, pl.ds(row, count - wide)], slot + 1)
            )
        slot += 2
    late = [
        start(res_pol, residual.at[:tokens], 4),
        start(res_ref, residual.at[tokens:], 5),
    ]
    for mask in range(count_s):
        place = lax.bitwise_xor(seq_index, mask)
        late.append(start(mod_pieces[mask], mod_hold.at[place], slot + mask))
    for copy in first:
        copy.wait()
    for step in range(count_f):
        for copy in blocks[step]:
            copy.wait()
        at = lax.rem(fsdp_index - step + count_f, count_f)
        proj[at] = dot(rows[...], base[at])
    for copy in smalls + late:
        copy.wait()
    mod_part = mod_hold.shape[2]
    for place in range(count_s):
        mod[:, place * mod_part : (place + 1) * mod_part] = mod_hold[place]

    def up_of(g):
        return small[g, :rank]

    def head_of(g, policy):
        first_row = rank + (channels if policy else 0)
        return small[g, first_row : first_row + channels]

    def down_of(g):
        return small[g, rank + 2 * channels :, :down_block]

    def columns(g):
        return slice(g * block, (g + 1) * block)

    def gate_of(g):
        return mod[:, g * block : (g + 1) * block]

    def shift_of(g):
        return mod[:, width + g * block : width + (g + 1) * block]

    def scale_of(g):
        return 1.0 + mod[:, 2 * width + g * block : 2 * width + (g + 1) * block]

    low = jnp.zeros((tokens, rank), jnp.float32)
    for g in range(count_f):
        low = low + contracted_columns(
            rows[:tokens, g * down_block : (g + 1) * down_block], down_of(g)
        )
    low_rows = low.astype(jnp.bfloat16)
    row_sum = jnp.zeros((2 * tokens, 1), jnp.float32)
    for g in range(count_f):
        proj[g, :tokens] = proj[g, :tokens] + dot(low_rows, up_of(g))
        stream = residual[:, columns(g)].astype(jnp.float32) + gate_of(g) * proj[g]
        proj[g] = stream
        row_sum = row_sum + jnp.sum(stream, axis=1, keepdims=True)
    mean = row_sum / width
    square_sum = jnp.zeros((2 * tokens, 1), jnp.float32)
    for g in range(count_f):
        centred = proj[g] - mean
        square_sum = square_sum + jnp.sum(centred * centred, axis=1, keepdims=True)
    inv_std = lax.rsqrt(square_sum / width + EPSILON)
    pred_pol = jnp.zeros((tokens, channels), jnp.float32)
    pred_ref = jnp.zeros((tokens, channels), jnp.float32)
    for g in range(count_f):
        normed = (proj[g] - mean) * inv_std
        proj[g] = normed
        z_rows = (normed * scale_of(g) + shift_of(g)).astype(jnp.bfloat16)
        z_hold[g] = z_rows[:tokens]
        pred_pol = pred_pol + contracted_columns(z_rows[:tokens], head_of(g, True))
        pred_ref = pred_ref + contracted_columns(z_rows[tokens:], head_of(g, False))
    target = noise[...] - latent[...]
    half_rows = lax.broadcasted_iota(jnp.int32, (tokens, channels), 0) < tokens // 2
    sign = jnp.where(half_rows, 1.0, -1.0)
    off_pol, off_ref = pred_pol - target, pred_ref - target
    local_margin = jnp.sum(sign * (off_pol * off_pol - off_ref * off_ref)) / scale_total
    lanes = margin_lanes(
        jnp.full((rank // 2, 128), local_margin, jnp.float32),
        seq_index,
        lambda value: value.astype(jnp.bfloat16).astype(jnp.float32),
    ).astype(jnp.bfloat16)
    for g in range(count_f):
        keep[g, :, down_block + 2 * block :] = lanes
        send[g, :, down_block + 2 * block :] = lanes
    dpred_wide = 2.0 * sign * off_pol
    dpred = dpred_wide.astype(jnp.bfloat16)
    dpred_turned = dpred_wide.T.astype(jnp.bfloat16)
    low_turned = low.T.astype(jnp.bfloat16)
    sum_dn = jnp.zeros((tokens, 1), jnp.float32)
    sum_dn_normed = jnp.zeros((tokens, 1), jnp.float32)
    half = rank // 2
    core = lax.rem(seq_index, 2)

    def put(g, first_column, value):
        value = value.astype(jnp.bfloat16).astype(jnp.float32)
        last_column = first_column + value.shape[1]
        top, bottom = value[:half], value[half:]
        keep[g, :, first_column:last_column] = jnp.where(core == 0, top, bottom).astype(jnp.bfloat16)
        send[g, :, first_column:last_column] = jnp.where(core == 0, bottom, top).astype(jnp.bfloat16)

    for g in range(count_f):
        put(g, down_block + block, dot(dpred_turned, z_hold[g]))
        dn_rows = dot(dpred, head_of(g, True)) * scale_of(g)
        back[g] = dn_rows
        sum_dn = sum_dn + jnp.sum(dn_rows, axis=1, keepdims=True)
        sum_dn_normed = sum_dn_normed + jnp.sum(dn_rows * proj[g, :tokens], axis=1, keepdims=True)
    mean_dn, mean_dn_normed = sum_dn / width, sum_dn_normed / width
    inv_pol = inv_std[:tokens]
    low_grad = jnp.zeros((tokens, rank), jnp.float32)
    for g in range(count_f):
        dstream = inv_pol * (back[g] - mean_dn - proj[g, :tokens] * mean_dn_normed)
        dstream_out[:, columns(g)] = dstream
        dproj_rows = (gate_of(g) * dstream).astype(jnp.bfloat16)
        dproj[g] = dproj_rows
        put(g, down_block, dot(low_turned, dproj_rows))
        low_grad = low_grad + contracted_columns(dproj_rows, up_of(g))
    low_grad_rows = low_grad.astype(jnp.bfloat16)
    low_grad_turned = low_grad.T.astype(jnp.bfloat16)
    for g in range(count_f):
        put(g, 0, dot(low_grad_turned, rows[:tokens, g * down_block : (g + 1) * down_block]))
    for g in range(count_f):
        at = slice(g * down_block, (g + 1) * down_block)
        value = dot(low_grad_rows, down_of(g))
        for other in range(count_f):
            value = value + contracted_columns(dproj[other], base[other, at])
        attn_out[:, at] = value


def step_call(where, operands, chunks, spans, tokens, features, width, rank, channels, scale_total):
    count_f, count_s = lax.axis_size("fsdp"), lax.axis_size("seq")
    sizes = (tokens, features, width, rank, channels, count_f, count_s, scale_total, spans)
    block = width // count_f
    grads = jax.ShapeDtypeStruct(
        (count_f, rank // 2, features // count_f + 2 * block + 128), jnp.bfloat16
    )
    any_space = pl.BlockSpec(memory_space=pl.ANY)
    vmem = pl.BlockSpec(memory_space=pltpu.VMEM)
    return pl.pallas_call(
        lambda *refs: step_kernel(sizes, *refs),
        out_shape=(
            grads,
            grads,
            jax.ShapeDtypeStruct((tokens, width), jnp.float32),
            jax.ShapeDtypeStruct((tokens, features), jnp.float32),
        ),
        in_specs=[pl.BlockSpec(memory_space=pltpu.SMEM)]
        + [any_space] * 4
        + [vmem] * 2
        + [any_space] * (len(operands) - 6 + len(chunks)),
        out_specs=(vmem,) * 4,
        scratch_shapes=[
            pltpu.VMEM((2 * tokens, features), jnp.bfloat16),
            pltpu.VMEM((count_f, features, block), jnp.bfloat16),
            pltpu.VMEM((count_f, 2 * rank + 2 * channels, block), jnp.bfloat16),
            pltpu.VMEM((2 * tokens, width), jnp.bfloat16),
            pltpu.VMEM((count_f, 2 * tokens, block), jnp.float32),
            pltpu.VMEM((count_f, tokens, block), jnp.bfloat16),
            pltpu.VMEM((count_f, tokens, block), jnp.float32),
            pltpu.VMEM((count_f, tokens, block), jnp.bfloat16),
            pltpu.VMEM((count_s, 1, 3 * width // count_s), jnp.float32),
            pltpu.VMEM((1, 3 * width), jnp.float32),
            pltpu.SemaphoreType.DMA((6 + 2 * len(chunks) + count_s,)),
        ],
        compiler_params=pltpu.CompilerParams(vmem_limit_bytes=60 * 1024 * 1024),
        name="step",
    )(where, *operands, *chunks)


def gather_chunks(own, own_small, seq_index):
    count_f, count_s = lax.axis_size("fsdp"), lax.axis_size("seq")
    part, small_part = own.shape[0] // count_s, own_small.shape[0] // count_s
    columns = own.shape[1]
    chunk = jnp.concatenate(
        [
            lax.dynamic_slice(own, (seq_index * part, 0), (part, columns)),
            lax.dynamic_slice(own_small, (seq_index * small_part, 0), (small_part, columns)),
        ],
        axis=0,
    )
    arrived = []
    for step in range(1, count_f):
        arrived.append(shift(chunk, step))
    middle = (part + small_part) // 32 * 16
    chunks, spans = [], []

    def add(step, mask, first_row, piece):
        chunks.extend([piece, swap(piece, 1)])
        spans.append((step, mask, first_row, piece.shape[0]))
        spans.append((step, mask + 1, first_row, piece.shape[0]))

    for step in range(1, count_f):
        held = arrived[step - 1]
        add(step, 0, 0, held)
        if count_s == 8:
            first, second = swap(held, 2), swap(held, 4)
            top, bottom = swap(first[:middle], 4), swap(second[middle:], 2)
            add(step, 2, 0, first)
            add(step, 4, 0, second)
            add(step, 6, 0, top)
            add(step, 6, middle, bottom)
        else:
            for mask in range(2, count_s, 2):
                add(step, mask, 0, swap(held, mask))
    return chunks, tuple(spans)


def dense_step(
    fsdp_index,
    seq_index,
    reference_attention,
    policy_attention,
    reference_residual,
    policy_residual,
    noise,
    latent,
    modulation,
    frozen_output_weight,
    small_weights,
    rank,
    scale_total,
):
    feature_index, block = frozen_output_weight.shape
    tokens, layer_width = reference_residual.shape
    channel_count = noise.shape[1]
    count_f = lax.axis_size("fsdp")
    down_block = feature_index // count_f
    gate_row = modulation[:, :layer_width]
    shift_row = modulation[:, layer_width : 2 * layer_width]
    scale_row = modulation[:, 2 * layer_width :]
    ext = jnp.concatenate([frozen_output_weight, small_weights], axis=0)
    full = gather_weights(ext, fsdp_index, seq_index)
    base_full = full[:feature_index]
    up_full = full[feature_index : feature_index + rank]
    head_ref_full = full[feature_index + rank : feature_index + rank + channel_count]
    head_pol_full = full[feature_index + rank + channel_count : feature_index + rank + 2 * channel_count]
    down_full = (
        full[feature_index + rank + 2 * channel_count :]
        .reshape(rank, count_f, block)[:, :, :down_block]
        .reshape(rank, feature_index)
    )

    rows_ref, policy_rows = reference_attention, policy_attention
    stream_ref, stream_pol = reference_residual, policy_residual
    target = noise - latent
    tok_seq = tokens // 2
    sign_rows = jnp.concatenate(
        [jnp.ones((tok_seq, 1), jnp.float32), -jnp.ones((tok_seq, 1), jnp.float32)], axis=0
    )
    proj_ref = jnp.dot(rows_ref, base_full, preferred_element_type=jnp.float32)
    _, _, _, pred_ref = final_layer(
        proj_ref, stream_ref, gate_row, shift_row, scale_row, head_ref_full
    )
    part_ref = member_errors(pred_ref, target, scale_total)
    low_rank_rows = contracted_columns(policy_rows, down_full).astype(jnp.bfloat16)
    policy_projection = jnp.dot(
        policy_rows, base_full, preferred_element_type=jnp.float32
    ) + jnp.dot(low_rank_rows, up_full, preferred_element_type=jnp.float32)
    normed_pol, inv_pol, z_pol, pred_pol = final_layer(
        policy_projection, stream_pol, gate_row, shift_row, scale_row, head_pol_full
    )
    part_pol = member_errors(pred_pol, target, scale_total)
    local_margin = part_pol[0] - part_ref[0] - (part_pol[1] - part_ref[1])
    lanes = margin_lanes(
        jnp.full((rank, 128), local_margin, jnp.float32),
        seq_index,
        lambda value: lax.reduce_precision(value, 8, 7),
    ).astype(jnp.bfloat16)

    dpred = (sign_rows * 2.0 * (pred_pol - target)).astype(jnp.bfloat16)
    head_part = contract_rows(dpred, z_pol)
    dz_rows = jnp.dot(dpred, head_pol_full, preferred_element_type=jnp.float32)
    dn_rows = dz_rows * (1.0 + scale_row)
    dstream = inv_pol * (
        dn_rows
        - jnp.mean(dn_rows, axis=1, keepdims=True)
        - normed_pol * jnp.mean(dn_rows * normed_pol, axis=1, keepdims=True)
    )
    projection_gradient = (gate_row * dstream).astype(jnp.bfloat16)
    up_part = contract_rows(low_rank_rows, projection_gradient)
    low_rank_gradient = contracted_columns(projection_gradient, up_full).astype(jnp.bfloat16)
    down_part = contract_rows(low_rank_gradient, policy_rows)
    attn = contracted_columns(projection_gradient, base_full) + jnp.dot(
        low_rank_gradient, down_full, preferred_element_type=jnp.float32
    )

    def blocks(value):
        return value.astype(jnp.bfloat16).reshape(value.shape[0], count_f, -1).transpose(1, 0, 2)

    lanes = jnp.broadcast_to(lanes[None], (count_f,) + lanes.shape)
    grads = jnp.concatenate([blocks(down_part), blocks(up_part), blocks(head_part), lanes], axis=2)
    grads = grads.reshape(count_f, 2, rank // 2, -1)
    core = seq_index % 2
    return (pick(grads, core, 1), pick(grads, 1 - core, 1), dstream, attn)


def local(
    timestep,
    pooled,
    modulation_weight,
    reference_attention,
    policy_attention,
    reference_residual,
    policy_residual,
    noise,
    latent,
    frozen_output_weight,
    adapter_down_weight,
    adapter_up_weight,
    reference_head,
    policy_head,
):
    layer_width = pooled.shape[1]
    feature_index = reference_attention.shape[-1]
    channel_count = noise.shape[-1]
    rank = adapter_down_weight.shape[0]
    tok_seq = reference_attention.shape[2]
    count_f, count_s = lax.axis_size("fsdp"), lax.axis_size("seq")
    fsdp_index, seq_index = lax.axis_index("fsdp"), lax.axis_index("seq")
    length = tok_seq * count_s
    scale_total = float(length * channel_count)
    beta = math.sqrt(length * channel_count) / 8.0

    cond_vec = pooled.astype(jnp.float32) + embedding(timestep, layer_width)
    activated = jax.nn.silu(cond_vec).astype(jnp.bfloat16)
    by_block = activated.reshape(pooled.shape[0], count_f, -1).transpose(1, 0, 2)
    pieces = [pick(by_block, fsdp_index)]
    for step in range(1, count_f):
        pieces.append(shift(pick(by_block, (fsdp_index + step) % count_f), step))
    per_pair = pooled.shape[0]
    partial_value = jnp.dot(
        jnp.concatenate(pieces, axis=0), modulation_weight, preferred_element_type=jnp.float32
    )
    own_part = partial_value[:per_pair]
    for step in range(1, count_f):
        own_part = own_part + shift(
            partial_value[per_pair * step : per_pair * (step + 1)], count_f - step
        )
    mod_plane = [own_part] + [swap(own_part, 2 * mask) for mask in range(1, count_s // 2)]
    mod_pieces = []
    for piece in mod_plane:
        mod_pieces += [piece, swap(piece, 1)]

    block = frozen_output_weight.shape[1]
    down_block = adapter_down_weight.shape[1]
    small_weights = jnp.concatenate(
        [
            adapter_up_weight,
            reference_head,
            policy_head,
            jnp.pad(adapter_down_weight, ((0, 0), (0, block - down_block))),
        ],
        axis=0,
    )
    tokens = 2 * tok_seq
    inputs = (
        policy_attention.reshape(tokens, feature_index),
        reference_attention.reshape(tokens, feature_index),
        policy_residual.reshape(tokens, layer_width),
        reference_residual.reshape(tokens, layer_width),
        noise.reshape(tokens, channel_count),
        latent.reshape(tokens, channel_count),
        frozen_output_weight,
        small_weights,
        *mod_pieces,
    )
    part, small_part = feature_index // count_s, small_weights.shape[0] // count_s
    if down_block % 128 or block % 128 or part % 16 or small_part % 16 or rank % 32:
        keep, send, dstream, attn = dense_step(
            fsdp_index,
            seq_index,
            inputs[1],
            inputs[0],
            inputs[3],
            inputs[2],
            *inputs[4:6],
            in_order(mod_pieces, seq_index).reshape(1, -1),
            frozen_output_weight,
            small_weights,
            rank,
            scale_total,
        )
    else:
        keep, send, dstream, attn = step_call(
            jnp.stack([fsdp_index, seq_index]).astype(jnp.int32),
            inputs,
            *gather_chunks(frozen_output_weight, small_weights, seq_index),
            tokens,
            feature_index,
            layer_width,
            rank,
            channel_count,
            scale_total,
        )

    plane_count, plane_index = count_s // 2, seq_index // 2
    width = keep.shape[2] - 128
    half = (keep.astype(jnp.float32) + swap(send, 1).astype(jnp.float32)).astype(jnp.bfloat16)
    half = half.reshape(count_f, plane_count, rank // count_s, width + 128)
    total = pick(half, plane_index, 1).astype(jnp.float32)
    for mask in range(1, plane_count):
        total = total + swap(pick(half, plane_index ^ mask, 1), 2 * mask).astype(jnp.float32)
    margin = jnp.sum(total[0, 0, width:])
    loss = jax.nn.softplus(beta * margin).reshape(1)
    weight_pair = jax.nn.sigmoid(beta * margin)
    grad_resid = (weight_pair * dstream).astype(jnp.bfloat16).reshape(policy_residual.shape)
    grad_attn = (weight_pair * attn).astype(jnp.bfloat16).reshape(policy_attention.shape)
    pair_sum = (weight_pair * total[:, :, :width]).astype(jnp.bfloat16)
    own_sum = pick(pair_sum, fsdp_index).astype(jnp.float32)
    for step in range(1, count_f):
        own_sum = own_sum + shift(pick(pair_sum, (fsdp_index + step) % count_f), step).astype(
            jnp.float32
        )
    gathered = gather_seq(own_sum.astype(jnp.bfloat16), seq_index)
    gathered = gathered.reshape(plane_count, 2, rank // count_s, width).transpose(1, 0, 2, 3)
    sums = gathered.reshape(rank, width).astype(jnp.float32)
    square = jnp.full((8, 128), jnp.sum(sums * sums), jnp.float32)
    total_square = square
    for step in range(1, count_f):
        total_square = total_square + shift(square, step)
    upper_limit = math.sqrt(
        rank * feature_index + rank * layer_width + channel_count * layer_width
    )
    factor = jnp.minimum(1.0, upper_limit / jnp.sqrt(total_square[0, 0] + 1e-12))
    scaled = factor * sums
    return (
        loss,
        scaled[:, :down_block],
        scaled[:, down_block : down_block + block],
        scaled[:, down_block + block :],
        grad_resid,
        grad_attn,
    )


def solution(mesh):
    in_specs = (
        P("fsdp"),
        P("fsdp", None),
        P("fsdp", "seq"),
        P("fsdp", None, "seq", None),
        P("fsdp", None, "seq", None),
        P("fsdp", None, "seq", None),
        P("fsdp", None, "seq", None),
        P("fsdp", None, "seq", None),
        P("fsdp", None, "seq", None),
        P(None, "fsdp"),
        P(None, "fsdp"),
        P(None, "fsdp"),
        P(None, "fsdp"),
        P(None, "fsdp"),
    )
    out_specs = (
        P("fsdp"),
        P(None, "fsdp"),
        P(None, "fsdp"),
        P(None, "fsdp"),
        P("fsdp", None, "seq", None),
        P("fsdp", None, "seq", None),
    )

    return jax.shard_map(local, mesh=mesh, in_specs=in_specs, out_specs=out_specs, check_vma=False)
```

profile of v0, /device:TPU:0, one launch (start us, length us, event | category | flops | bytes accessed | tf_op | source)
XLA Modules:
  0.0 158.1 jit_solution(11150797644636685030)
XLA Ops:
  2.5 3.1 %collective-permute-start = (bf16[1,768]{1,0:T(2,128)(2,1)S(1)}, bf16[1,768]{1,0:T(2,128)(2,1)S(1)}, u32[]{:S(2)}, u32[]{:S(2)}) collective-permute-start(bf16[1,768]{1,0:T(2,128)(2,1)S(1)} %get-tuple-element.30), channel_id=1, source_target_pairs={{0,8},{8,16},{16,24},{24,0},{1,9},{9,17},{17,25},{25,1},{2,10},{10... | collective-permute-start | bytes 4616 | tf_op jit(solution)/shard_map/ppermute | solution.py:35
  5.6 2.6 %collective-permute-start.1 = (bf16[1,768]{1,0:T(2,128)(2,1)S(1)}, bf16[1,768]{1,0:T(2,128)(2,1)S(1)}, u32[]{:S(2)}, u32[]{:S(2)}) collective-permute-start(bf16[1,768]{1,0:T(2,128)(2,1)S(1)} %get-tuple-element.29), channel_id=1, source_target_pairs={{0,16},{8,24},{16,0},{24,8},{1,17},{9,25},{17,1},{25,9},{2,18},{10... | collective-permute-start | bytes 4616 | tf_op jit(solution)/shard_map/ppermute | solution.py:35
  13.2 2.9 %collective-permute-start.3 = (f32[1,1152]{1,0:T(1,128)S(1)}, f32[1,1152]{1,0:T(1,128)S(1)}, u32[]{:S(2)}, u32[]{:S(2)}) collective-permute-start(f32[1,1152]{1,0:T(1,128)S(1)} %get-tuple-element.24), channel_id=1, source_target_pairs={{0,24},{8,0},{16,8},{24,16},{1,25},{9,1},{17,9},{25,17},{2,26},{10... | collective-permute-start | bytes 13832 | tf_op jit(solution)/shard_map/ppermute | solution.py:35
  16.1 2.0 %collective-permute-start.4 = (f32[1,1152]{1,0:T(1,128)S(1)}, f32[1,1152]{1,0:T(1,128)S(1)}, u32[]{:S(2)}, u32[]{:S(2)}) collective-permute-start(f32[1,1152]{1,0:T(1,128)S(1)} %get-tuple-element.26), channel_id=1, source_target_pairs={{0,16},{8,24},{16,0},{24,8},{1,17},{9,25},{17,1},{25,9},{2,18},{10... | collective-permute-start | bytes 13832 | tf_op jit(solution)/shard_map/ppermute | solution.py:35
  18.1 8.5 %collective-permute-done.3 = f32[1,1152]{1,0:T(1,128)S(1)} collective-permute-done((f32[1,1152]{1,0:T(1,128)S(1)}, f32[1,1152]{1,0:T(1,128)S(1)}, u32[]{:S(2)}, u32[]{:S(2)}) %collective-permute-start.3) | collective-permute-done | bytes 4640 | tf_op jit(solution)/shard_map/ppermute | solution.py:35
  26.6 4.3 %collective-permute-start.33 = (bf16[224,768]{1,0:T(8,128)(2,1)S(1)}, bf16[224,768]{1,0:T(8,128)(2,1)S(1)}, u32[]{:S(2)}, u32[]{:S(2)}) collective-permute-start(bf16[224,768]{1,0:T(8,128)(2,1)S(1)} %pad_maximum_fusion), channel_id=1, source_target_pairs={{0,24},{8,0},{16,8},{24,16},{1,25},{9,1},{17,9},{25,17},{2,26},{10... | collective-permute-start | bytes 1032200 | tf_op jit(solution)/shard_map/ppermute | solution.py:35
  32.4 4.9 %collective-permute-done.4 = f32[1,1152]{1,0:T(1,128)S(1)} collective-permute-done((f32[1,1152]{1,0:T(1,128)S(1)}, f32[1,1152]{1,0:T(1,128)S(1)}, u32[]{:S(2)}, u32[]{:S(2)}) %collective-permute-start.4) | collective-permute-done | bytes 4640 | tf_op jit(solution)/shard_map/ppermute | solution.py:35
  40.9 6.0 %collective-permute-done.9.refs_13_ = f32[1,1152]{1,0:T(1,128)S(1)} collective-permute-done((f32[1,1152]{1,0:T(1,128)S(1)}, f32[1,1152]{1,0:T(1,128)S(1)}, u32[]{:S(2)}, u32[]{:S(2)}) %collective-permute-start.9) | collective-permute-done | bytes 4640 | tf_op jit(solution)/shard_map/ppermute | solution.py:40
  46.9 2.4 %collective-permute-start.11 = (f32[1,1152]{1,0:T(1,128)S(1)}, f32[1,1152]{1,0:T(1,128)S(1)}, u32[]{:S(2)}, u32[]{:S(2)}) collective-permute-start(f32[1,1152]{1,0:T(1,128)S(1)} %fusion.19.refs_9_), channel_id=1, source_target_pairs={{0,6},{1,7},{2,4},{3,5},{4,2},{5,3},{6,0},{7,1},{8,14},{9,15},{10,... | collective-permute-start | bytes 13832 | tf_op jit(solution)/shard_map/ppermute | solution.py:40
  49.3 2.1 %collective-permute-done.11.refs_15_ = f32[1,1152]{1,0:T(1,128)S(1)} collective-permute-done((f32[1,1152]{1,0:T(1,128)S(1)}, f32[1,1152]{1,0:T(1,128)S(1)}, u32[]{:S(2)}, u32[]{:S(2)}) %collective-permute-start.11) | collective-permute-done | bytes 4640 | tf_op jit(solution)/shard_map/ppermute | solution.py:40
  52.9 2.1 %collective-permute-done.7.refs_11_ = f32[1,1152]{1,0:T(1,128)S(1)} collective-permute-done((f32[1,1152]{1,0:T(1,128)S(1)}, f32[1,1152]{1,0:T(1,128)S(1)}, u32[]{:S(2)}, u32[]{:S(2)}) %collective-permute-start.7) | collective-permute-done | bytes 4640 | tf_op jit(solution)/shard_map/ppermute | solution.py:40
  63.7 6.9 %collective-permute-done.27.refs_31_ = bf16[224,768]{1,0:T(8,128)(2,1)S(1)} collective-permute-done((bf16[224,768]{1,0:T(8,128)(2,1)S(1)}, bf16[224,768]{1,0:T(8,128)(2,1)S(1)}, u32[]{:S(2)}, u32[]{:S(2)}) %collective-permute-start.27) | collective-permute-done | bytes 344096 | tf_op jit(solution)/shard_map/ppermute | solution.py:40
  72.3 5.7 %collective-permute-done.37.refs_41_ = bf16[224,768]{1,0:T(8,128)(2,1)S(1)} collective-permute-done((bf16[224,768]{1,0:T(8,128)(2,1)S(1)}, bf16[224,768]{1,0:T(8,128)(2,1)S(1)}, u32[]{:S(2)}, u32[]{:S(2)}) %collective-permute-start.37) | collective-permute-done | bytes 344096 | tf_op jit(solution)/shard_map/ppermute | solution.py:40
  86.4 2.4 %collective-permute-done.31.refs_35_ = bf16[112,768]{1,0:T(8,128)(2,1)S(1)} collective-permute-done((bf16[112,768]{1,0:T(8,128)(2,1)S(1)}, bf16[112,768]{1,0:T(8,128)(2,1)S(1)}, u32[]{:S(2)}, u32[]{:S(2)}) %collective-permute-start.31) | collective-permute-done | bytes 172064 | tf_op jit(solution)/shard_map/ppermute | solution.py:40
  96.2 14.5 %step.1 = (bf16[4,32,2048]{2,1,0:T(8,128)(2,1)}, bf16[4,32,2048]{2,1,0:T(8,128)(2,1)}, f32[128,3072]{1,0:T(8,128)}, f32[128,1536]{1,0:T(8,128)}) custom-call(s32[2]{0:T(128)} %pad_add_fusion.refs_0_, bf16[128,1536]{1,0:T(8,128)(2,1)} %bitcast.61, bf16[128,1536]{1,0:T(8,128)(2,1)} %bitcast.62, bf16[128,3072]{1,0:T(8,128)(2,1)} %bitcast.58, ...), custom_call_target="tpu_custom_call" | custom-call | tf_op jit(solution)/shard_map/step/pallas_call | solution.py:302
  111.0 1.8 %collective-permute-done.43 = bf16[4,32,2048]{2,1,0:T(8,128)(2,1)S(1)} collective-permute-done((bf16[4,32,2048]{2,1,0:T(8,128)(2,1)}, bf16[4,32,2048]{2,1,0:T(8,128)(2,1)S(1)}, u32[]{:S(2)}, u32[]{:S(2)}) %collective-permute-start.43) | collective-permute-done | bytes 524320 | tf_op jit(solution)/shard_map/ppermute | solution.py:40
  117.7 2.9 %collective-permute-done.44 = bf16[4,8,2048]{2,1,0:T(8,128)(2,1)S(1)} collective-permute-done((bf16[4,8,2048]{2,1,0:T(8,128)(2,1)S(1)}, bf16[4,8,2048]{2,1,0:T(8,128)(2,1)S(1)}, u32[]{:S(2)}, u32[]{:S(2)}) %collective-permute-start.44) | collective-permute-done | bytes 131104 | tf_op jit(solution)/shard_map/ppermute | solution.py:40
  120.5 2.7 %collective-permute-done.45 = bf16[4,8,2048]{2,1,0:T(8,128)(2,1)S(1)} collective-permute-done((bf16[4,8,2048]{2,1,0:T(8,128)(2,1)S(1)}, bf16[4,8,2048]{2,1,0:T(8,128)(2,1)S(1)}, u32[]{:S(2)}, u32[]{:S(2)}) %collective-permute-start.45) | collective-permute-done | bytes 131104 | tf_op jit(solution)/shard_map/ppermute | solution.py:40
  124.7 4.1 %collective-permute-start.47 = (bf16[8,1920]{1,0:T(8,128)(2,1)S(1)}, bf16[8,1920]{1,0:T(8,128)(2,1)S(1)}, u32[]{:S(2)}, u32[]{:S(2)}) collective-permute-start(bf16[8,1920]{1,0:T(8,128)(2,1)S(1)} %get-tuple-element.21), channel_id=1, source_target_pairs={{0,8},{8,16},{16,24},{24,0},{1,9},{9,17},{17,25},{25,1},{2,10},{10... | collective-permute-start | bytes 92168 | tf_op jit(solution)/shard_map/ppermute | solution.py:35
  128.8 2.6 %collective-permute-start.48 = (bf16[8,1920]{1,0:T(8,128)(2,1)S(1)}, bf16[8,1920]{1,0:T(8,128)(2,1)S(1)}, u32[]{:S(2)}, u32[]{:S(2)}) collective-permute-start(bf16[8,1920]{1,0:T(8,128)(2,1)S(1)} %get-tuple-element.23), channel_id=1, source_target_pairs={{0,16},{8,24},{16,0},{24,8},{1,17},{9,25},{17,1},{25,9},{2,18},{10... | collective-permute-start | bytes 92168 | tf_op jit(solution)/shard_map/ppermute | solution.py:35
  133.6 1.7 %collective-permute-done.49 = bf16[8,1920]{1,0:T(8,128)(2,1)S(1)} collective-permute-done((bf16[8,1920]{1,0:T(8,128)(2,1)S(1)}, bf16[8,1920]{1,0:T(8,128)(2,1)S(1)}, u32[]{:S(2)}, u32[]{:S(2)}) %collective-permute-start.49) | collective-permute-done | bytes 30752 | tf_op jit(solution)/shard_map/ppermute | solution.py:35
  140.6 1.7 %collective-permute-done.52 = bf16[8,1920]{1,0:T(8,128)(2,1)S(1)} collective-permute-done((bf16[8,1920]{1,0:T(8,128)(2,1)S(1)}, bf16[8,1920]{1,0:T(8,128)(2,1)S(1)}, u32[]{:S(2)}, u32[]{:S(2)}) %collective-permute-start.52) | collective-permute-done | bytes 30752 | tf_op jit(solution)/shard_map/ppermute | solution.py:40
  142.4 2.5 %multiply_convert_fusion = bf16[128,3072]{1,0:T(8,128)(2,1)} fusion(f32[128,3072]{1,0:T(8,128)} %get-tuple-element.12, f32[]{:T(128)S(6)} %div.30), kind=kLoop, calls=%fused_computation | loop fusion | flops 786432 | bytes 2359300 | tf_op jit(solution)/shard_map/convert_element_type | solution.py:569
  146.7 3.4 %collective-permute-start.55 = (f32[8,128]{1,0:T(8,128)S(1)}, f32[8,128]{1,0:T(8,128)S(1)}, u32[]{:S(2)}, u32[]{:S(2)}) collective-permute-start(f32[8,128]{1,0:T(8,128)S(1)} %broadcast_in_dim.2), channel_id=1, source_target_pairs={{0,16},{8,24},{16,0},{24,8},{1,17},{9,25},{17,1},{25,9},{2,18},{10... | collective-permute-start | bytes 12296 | tf_op jit(solution)/shard_map/ppermute | solution.py:35
  (224 shorter events, 59.6 us)
Async XLA Ops:
  2.5 10.3 %collective-permute-start = (bf16[1,768]{1,0:T(2,128)(2,1)S(1)}, bf16[1,768]{1,0:T(2,128)(2,1)S(1)}, u32[]{:S(2)}, u32[]{:S(2)}) collective-permute-start(bf16[1,768]{1,0:T(2,128)(2,1)S(1)} %get-tuple-element.30), channel_id=1, source_target_pairs={{0,8},{8,16},{16,24},{24,0},{1,9},{9,17},{17,25},{25,1},{2,10},{10... | collective-permute-start | bytes 4616 | tf_op jit(solution)/shard_map/ppermute | solution.py:35
  5.6 7.2 %collective-permute-start.1 = (bf16[1,768]{1,0:T(2,128)(2,1)S(1)}, bf16[1,768]{1,0:T(2,128)(2,1)S(1)}, u32[]{:S(2)}, u32[]{:S(2)}) collective-permute-start(bf16[1,768]{1,0:T(2,128)(2,1)S(1)} %get-tuple-element.29), channel_id=1, source_target_pairs={{0,16},{8,24},{16,0},{24,8},{1,17},{9,25},{17,1},{25,9},{2,18},{10... | collective-permute-start | bytes 4616 | tf_op jit(solution)/shard_map/ppermute | solution.py:35
  11.8 19.1 %collective-permute-start.13 = (bf16[224,768]{1,0:T(8,128)(2,1)S(1)}, bf16[224,768]{1,0:T(8,128)(2,1)S(1)}, u32[]{:S(2)}, u32[]{:S(2)}) collective-permute-start(bf16[224,768]{1,0:T(8,128)(2,1)S(1)} %pad_maximum_fusion), channel_id=1, source_target_pairs={{0,8},{8,16},{16,24},{24,0},{1,9},{9,17},{17,25},{25,1},{2,10},{10... | collective-permute-start | bytes 1032200 | tf_op jit(solution)/shard_map/ppermute | solution.py:35
  12.5 26.3 %collective-permute-start.23 = (bf16[224,768]{1,0:T(8,128)(2,1)S(1)}, bf16[224,768]{1,0:T(8,128)(2,1)S(1)}, u32[]{:S(2)}, u32[]{:S(2)}) collective-permute-start(bf16[224,768]{1,0:T(8,128)(2,1)S(1)} %pad_maximum_fusion), channel_id=1, source_target_pairs={{0,16},{8,24},{16,0},{24,8},{1,17},{9,25},{17,1},{25,9},{2,18},{10... | collective-permute-start | bytes 1032200 | tf_op jit(solution)/shard_map/ppermute | solution.py:35
  13.2 13.4 %collective-permute-start.3 = (f32[1,1152]{1,0:T(1,128)S(1)}, f32[1,1152]{1,0:T(1,128)S(1)}, u32[]{:S(2)}, u32[]{:S(2)}) collective-permute-start(f32[1,1152]{1,0:T(1,128)S(1)} %get-tuple-element.24), channel_id=1, source_target_pairs={{0,24},{8,0},{16,8},{24,16},{1,25},{9,1},{17,9},{25,17},{2,26},{10... | collective-permute-start | bytes 13832 | tf_op jit(solution)/shard_map/ppermute | solution.py:35
  16.1 21.2 %collective-permute-start.4 = (f32[1,1152]{1,0:T(1,128)S(1)}, f32[1,1152]{1,0:T(1,128)S(1)}, u32[]{:S(2)}, u32[]{:S(2)}) collective-permute-start(f32[1,1152]{1,0:T(1,128)S(1)} %get-tuple-element.26), channel_id=1, source_target_pairs={{0,16},{8,24},{16,0},{24,8},{1,17},{9,25},{17,1},{25,9},{2,18},{10... | collective-permute-start | bytes 13832 | tf_op jit(solution)/shard_map/ppermute | solution.py:35
  18.1 22.2 %collective-permute-start.5 = (f32[1,1152]{1,0:T(1,128)S(1)}, f32[1,1152]{1,0:T(1,128)S(1)}, u32[]{:S(2)}, u32[]{:S(2)}) collective-permute-start(f32[1,1152]{1,0:T(1,128)S(1)} %get-tuple-element.25), channel_id=1, source_target_pairs={{0,8},{8,16},{16,24},{24,0},{1,9},{9,17},{17,25},{25,1},{2,10},{10... | collective-permute-start | bytes 13832 | tf_op jit(solution)/shard_map/ppermute | solution.py:35
  26.6 34.6 %collective-permute-start.33 = (bf16[224,768]{1,0:T(8,128)(2,1)S(1)}, bf16[224,768]{1,0:T(8,128)(2,1)S(1)}, u32[]{:S(2)}, u32[]{:S(2)}) collective-permute-start(bf16[224,768]{1,0:T(8,128)(2,1)S(1)} %pad_maximum_fusion), channel_id=1, source_target_pairs={{0,24},{8,0},{16,8},{24,16},{1,25},{9,1},{17,9},{25,17},{2,26},{10... | collective-permute-start | bytes 1032200 | tf_op jit(solution)/shard_map/ppermute | solution.py:35
  30.9 31.8 %collective-permute-start.15 = (bf16[224,768]{1,0:T(8,128)(2,1)S(1)}, bf16[224,768]{1,0:T(8,128)(2,1)S(1)}, u32[]{:S(2)}, u32[]{:S(2)}) collective-permute-start(bf16[224,768]{1,0:T(8,128)(2,1)S(1)} %collective-permute-done.13.refs_17_), channel_id=1, source_target_pairs={{0,2},{1,3},{2,0},{3,1},{4,6},{5,7},{6,4},{7,5},{8,10},{9,11},{10,... | collective-permute-start | bytes 1032200 | tf_op jit(solution)/shard_map/ppermute | solution.py:40
  37.3 25.9 %collective-permute-start.17 = (bf16[224,768]{1,0:T(8,128)(2,1)S(1)}, bf16[224,768]{1,0:T(8,128)(2,1)S(1)}, u32[]{:S(2)}, u32[]{:S(2)}) collective-permute-start(bf16[224,768]{1,0:T(8,128)(2,1)S(1)} %collective-permute-done.13.refs_17_), channel_id=1, source_target_pairs={{0,4},{1,5},{2,6},{3,7},{4,0},{5,1},{6,2},{7,3},{8,12},{9,13},{10,... | collective-permute-start | bytes 1032200 | tf_op jit(solution)/shard_map/ppermute | solution.py:40
  38.8 24.4 %collective-permute-start.25 = (bf16[224,768]{1,0:T(8,128)(2,1)S(1)}, bf16[224,768]{1,0:T(8,128)(2,1)S(1)}, u32[]{:S(2)}, u32[]{:S(2)}) collective-permute-start(bf16[224,768]{1,0:T(8,128)(2,1)S(1)} %collective-permute-done.23.refs_27_), channel_id=1, source_target_pairs={{0,2},{1,3},{2,0},{3,1},{4,6},{5,7},{6,4},{7,5},{8,10},{9,11},{10,... | collective-permute-start | bytes 1032200 | tf_op jit(solution)/shard_map/ppermute | solution.py:40
  59.7 10.9 %collective-permute-start.27 = (bf16[224,768]{1,0:T(8,128)(2,1)S(1)}, bf16[224,768]{1,0:T(8,128)(2,1)S(1)}, u32[]{:S(2)}, u32[]{:S(2)}) collective-permute-start(bf16[224,768]{1,0:T(8,128)(2,1)S(1)} %collective-permute-done.23.refs_27_), channel_id=1, source_target_pairs={{0,4},{1,5},{2,6},{3,7},{4,0},{5,1},{6,2},{7,3},{8,12},{9,13},{10,... | collective-permute-start | bytes 1032200 | tf_op jit(solution)/shard_map/ppermute | solution.py:40
  61.2 9.9 %collective-permute-start.35 = (bf16[224,768]{1,0:T(8,128)(2,1)S(1)}, bf16[224,768]{1,0:T(8,128)(2,1)S(1)}, u32[]{:S(2)}, u32[]{:S(2)}) collective-permute-start(bf16[224,768]{1,0:T(8,128)(2,1)S(1)} %collective-permute-done.33.refs_37_), channel_id=1, source_target_pairs={{0,2},{1,3},{2,0},{3,1},{4,6},{5,7},{6,4},{7,5},{8,10},{9,11},{10,... | collective-permute-start | bytes 1032200 | tf_op jit(solution)/shard_map/ppermute | solution.py:40
  62.7 15.3 %collective-permute-start.37 = (bf16[224,768]{1,0:T(8,128)(2,1)S(1)}, bf16[224,768]{1,0:T(8,128)(2,1)S(1)}, u32[]{:S(2)}, u32[]{:S(2)}) collective-permute-start(bf16[224,768]{1,0:T(8,128)(2,1)S(1)} %collective-permute-done.33.refs_37_), channel_id=1, source_target_pairs={{0,4},{1,5},{2,6},{3,7},{4,0},{5,1},{6,2},{7,3},{8,12},{9,13},{10,... | collective-permute-start | bytes 1032200 | tf_op jit(solution)/shard_map/ppermute | solution.py:40
  63.2 16.3 %collective-permute-start.14 = (bf16[224,768]{1,0:T(8,128)(2,1)S(1)}, bf16[224,768]{1,0:T(8,128)(2,1)S(1)}, u32[]{:S(2)}, u32[]{:S(2)}) collective-permute-start(bf16[224,768]{1,0:T(8,128)(2,1)S(1)} %collective-permute-done.13.refs_17_), channel_id=1, source_target_pairs={{0,1},{1,0},{2,3},{3,2},{4,5},{5,4},{6,7},{7,6},{8,9},{9,8},{10,11... | collective-permute-start | bytes 1032200 | tf_op jit(solution)/shard_map/ppermute | solution.py:40
  63.2 17.8 %collective-permute-start.24 = (bf16[224,768]{1,0:T(8,128)(2,1)S(1)}, bf16[224,768]{1,0:T(8,128)(2,1)S(1)}, u32[]{:S(2)}, u32[]{:S(2)}) collective-permute-start(bf16[224,768]{1,0:T(8,128)(2,1)S(1)} %collective-permute-done.23.refs_27_), channel_id=1, source_target_pairs={{0,1},{1,0},{2,3},{3,2},{4,5},{5,4},{6,7},{7,6},{8,9},{9,8},{10,11... | collective-permute-start | bytes 1032200 | tf_op jit(solution)/shard_map/ppermute | solution.py:40
  70.6 11.1 %collective-permute-start.34 = (bf16[224,768]{1,0:T(8,128)(2,1)S(1)}, bf16[224,768]{1,0:T(8,128)(2,1)S(1)}, u32[]{:S(2)}, u32[]{:S(2)}) collective-permute-start(bf16[224,768]{1,0:T(8,128)(2,1)S(1)} %collective-permute-done.33.refs_37_), channel_id=1, source_target_pairs={{0,1},{1,0},{2,3},{3,2},{4,5},{5,4},{6,7},{7,6},{8,9},{9,8},{10,11... | collective-permute-start | bytes 1032200 | tf_op jit(solution)/shard_map/ppermute | solution.py:40
  71.0 11.2 %collective-permute-start.19 = (bf16[112,768]{1,0:T(8,128)(2,1)S(1)}, bf16[112,768]{1,0:T(8,128)(2,1)S(1)}, u32[]{:S(2)}, u32[]{:S(2)}) collective-permute-start(bf16[112,768]{1,0:T(8,128)(2,1)S(1)} %slice.84), channel_id=1, source_target_pairs={{0,4},{1,5},{2,6},{3,7},{4,0},{5,1},{6,2},{7,3},{8,12},{9,13},{10,... | collective-permute-start | bytes 516104 | tf_op jit(solution)/shard_map/ppermute | solution.py:40
  78.0 7.2 %collective-permute-start.21 = (bf16[112,768]{1,0:T(8,128)(2,1)S(1)}, bf16[112,768]{1,0:T(8,128)(2,1)S(1)}, u32[]{:S(2)}, u32[]{:S(2)}) collective-permute-start(bf16[112,768]{1,0:T(8,128)(2,1)S(1)} %slice.85), channel_id=1, source_target_pairs={{0,2},{1,3},{2,0},{3,1},{4,6},{5,7},{6,4},{7,5},{8,10},{9,11},{10,... | collective-permute-start | bytes 516104 | tf_op jit(solution)/shard_map/ppermute | solution.py:40
  81.0 7.8 %collective-permute-start.31 = (bf16[112,768]{1,0:T(8,128)(2,1)S(1)}, bf16[112,768]{1,0:T(8,128)(2,1)S(1)}, u32[]{:S(2)}, u32[]{:S(2)}) collective-permute-start(bf16[112,768]{1,0:T(8,128)(2,1)S(1)} %slice.87), channel_id=1, source_target_pairs={{0,2},{1,3},{2,0},{3,1},{4,6},{5,7},{6,4},{7,5},{8,10},{9,11},{10,... | collective-permute-start | bytes 516104 | tf_op jit(solution)/shard_map/ppermute | solution.py:40
  81.7 7.1 %collective-permute-start.39 = (bf16[112,768]{1,0:T(8,128)(2,1)S(1)}, bf16[112,768]{1,0:T(8,128)(2,1)S(1)}, u32[]{:S(2)}, u32[]{:S(2)}) collective-permute-start(bf16[112,768]{1,0:T(8,128)(2,1)S(1)} %slice.88), channel_id=1, source_target_pairs={{0,4},{1,5},{2,6},{3,7},{4,0},{5,1},{6,2},{7,3},{8,12},{9,13},{10,... | collective-permute-start | bytes 516104 | tf_op jit(solution)/shard_map/ppermute | solution.py:40
  82.3 8.5 %collective-permute-start.41 = (bf16[112,768]{1,0:T(8,128)(2,1)S(1)}, bf16[112,768]{1,0:T(8,128)(2,1)S(1)}, u32[]{:S(2)}, u32[]{:S(2)}) collective-permute-start(bf16[112,768]{1,0:T(8,128)(2,1)S(1)} %slice.89), channel_id=1, source_target_pairs={{0,2},{1,3},{2,0},{3,1},{4,6},{5,7},{6,4},{7,5},{8,10},{9,11},{10,... | collective-permute-start | bytes 516104 | tf_op jit(solution)/shard_map/ppermute | solution.py:40
  115.1 8.2 %collective-permute-start.45 = (bf16[4,8,2048]{2,1,0:T(8,128)(2,1)S(1)}, bf16[4,8,2048]{2,1,0:T(8,128)(2,1)S(1)}, u32[]{:S(2)}, u32[]{:S(2)}) collective-permute-start(bf16[4,8,2048]{2,1,0:T(8,128)(2,1)S(1)} %get-tuple-element.18), channel_id=1, source_target_pairs={{0,4},{1,5},{2,6},{3,7},{4,0},{5,1},{6,2},{7,3},{8,12},{9,13},{10,... | collective-permute-start | bytes 393224 | tf_op jit(solution)/shard_map/ppermute | solution.py:40
  124.7 8.3 %collective-permute-start.47 = (bf16[8,1920]{1,0:T(8,128)(2,1)S(1)}, bf16[8,1920]{1,0:T(8,128)(2,1)S(1)}, u32[]{:S(2)}, u32[]{:S(2)}) collective-permute-start(bf16[8,1920]{1,0:T(8,128)(2,1)S(1)} %get-tuple-element.21), channel_id=1, source_target_pairs={{0,8},{8,16},{16,24},{24,0},{1,9},{9,17},{17,25},{25,1},{2,10},{10... | collective-permute-start | bytes 92168 | tf_op jit(solution)/shard_map/ppermute | solution.py:35
  (74 other events, 960.5 us)
where the time goes:
time: 159 us; the launch traced here: 158 us
  waiting for transfers between devices  64.3 us (40%)
  starting transfers between devices  59.8 us (38%)
  Pallas kernels  14.5 us (9%)
  other arithmetic  9.29 us (6%)
  local copies, waits for them, and re-layouts  5.13 us (3%)
  between operations  4.7 us (3%)
    ppermute x42, waiting for transfers between devices, swap(): return lax.ppermute(value, 'seq', [(i, i ^ mask) for i in range(count)])  46.1 us
    ppermute x42, starting transfers between devices, swap(): return lax.ppermute(value, 'seq', [(i, i ^ mask) for i in range(count)])  30.5 us
    ppermute x15, starting transfers between devices, shift(): lax.ppermute(value, 'fsdp', [(i, (i + step) % count) for i in range(count)])  29.3 us
    ppermute x15, waiting for transfers between devices, shift(): lax.ppermute(value, 'fsdp', [(i, (i + step) % count) for i in range(count)])  18.2 us
    pallas_call x1, Pallas kernels, step_call(): pl.pallas_call(lambda *refs: step_kernel(sizes, *refs), out_shape=(grads,...  14.5 us
  transfers between devices with their start and end apart: 57, of which 32 were waited for; matrix products, arithmetic and copies ran while one was open for 4% of the time, Pallas kernels for 0%

commit v1 on v0

--- a/solution.py
+++ b/solution.py
@@ -126,7 +126,7 @@
     )
 
 
-def step_kernel(sizes, where, *refs):
+def step_kernel(sizes, *refs):
     tokens, features, width, rank, channels, count_f, count_s, scale_total, spans = sizes
     block, down_block = width // count_f, features // count_f
     part, small_part = features // count_s, (2 * rank + 2 * channels) // count_s
@@ -135,7 +135,7 @@
     chunks, refs = refs[: len(spans)], refs[len(spans) :]
     keep, send, dstream_out, attn_out, refs = *refs[:4], refs[4:]
     rows, base, small, residual, proj, z_hold, back, dproj, mod_hold, mod, sems = refs
-    fsdp_index, seq_index = where[0], where[1]
+    fsdp_index, seq_index = lax.axis_index("fsdp"), lax.axis_index("seq")
 
     def start(source, target, slot):
         copy = pltpu.make_async_copy(source, target, sems.at[slot])
@@ -290,7 +290,7 @@
         attn_out[:, at] = value
 
 
-def step_call(where, operands, chunks, spans, tokens, features, width, rank, channels, scale_total):
+def step_call(operands, chunks, spans, tokens, features, width, rank, channels, scale_total):
     count_f, count_s = lax.axis_size("fsdp"), lax.axis_size("seq")
     sizes = (tokens, features, width, rank, channels, count_f, count_s, scale_total, spans)
     block = width // count_f
@@ -307,8 +307,7 @@
             jax.ShapeDtypeStruct((tokens, width), jnp.float32),
             jax.ShapeDtypeStruct((tokens, features), jnp.float32),
         ),
-        in_specs=[pl.BlockSpec(memory_space=pltpu.SMEM)]
-        + [any_space] * 4
+        in_specs=[any_space] * 4
         + [vmem] * 2
         + [any_space] * (len(operands) - 6 + len(chunks)),
         out_specs=(vmem,) * 4,
@@ -327,10 +326,10 @@
         ],
         compiler_params=pltpu.CompilerParams(vmem_limit_bytes=60 * 1024 * 1024),
         name="step",
-    )(where, *operands, *chunks)
-
-
-def gather_chunks(own, own_small, seq_index):
+    )(*operands, *chunks)
+
+
+def send_chunks(own, own_small, seq_index):
     count_f, count_s = lax.axis_size("fsdp"), lax.axis_size("seq")
     part, small_part = own.shape[0] // count_s, own_small.shape[0] // count_s
     columns = own.shape[1]
@@ -344,6 +343,11 @@
     arrived = []
     for step in range(1, count_f):
         arrived.append(shift(chunk, step))
+    return arrived
+
+
+def spread_chunks(arrived, part, small_part):
+    count_f, count_s = lax.axis_size("fsdp"), lax.axis_size("seq")
     middle = (part + small_part) // 32 * 16
     chunks, spans = [], []
 
@@ -484,26 +488,6 @@
     scale_total = float(length * channel_count)
     beta = math.sqrt(length * channel_count) / 8.0
 
-    cond_vec = pooled.astype(jnp.float32) + embedding(timestep, layer_width)
-    activated = jax.nn.silu(cond_vec).astype(jnp.bfloat16)
-    by_block = activated.reshape(pooled.shape[0], count_f, -1).transpose(1, 0, 2)
-    pieces = [pick(by_block, fsdp_index)]
-    for step in range(1, count_f):
-        pieces.append(shift(pick(by_block, (fsdp_index + step) % count_f), step))
-    per_pair = pooled.shape[0]
-    partial_value = jnp.dot(
-        jnp.concatenate(pieces, axis=0), modulation_weight, preferred_element_type=jnp.float32
-    )
-    own_part = partial_value[:per_pair]
-    for step in range(1, count_f):
-        own_part = own_part + shift(
-            partial_value[per_pair * step : per_pair * (step + 1)], count_f - step
-        )
-    mod_plane = [own_part] + [swap(own_part, 2 * mask) for mask in range(1, count_s // 2)]
-    mod_pieces = []
-    for piece in mod_plane:
-        mod_pieces += [piece, swap(piece, 1)]
-
     block = frozen_output_weight.shape[1]
     down_block = adapter_down_weight.shape[1]
     small_weights = jnp.concatenate(
@@ -515,6 +499,35 @@
         ],
         axis=0,
     )
+    part, small_part = feature_index // count_s, small_weights.shape[0] // count_s
+    dense = down_block % 128 or block % 128 or part % 16 or small_part % 16 or rank % 32
+    if not dense:
+        arrived = send_chunks(frozen_output_weight, small_weights, seq_index)
+        chunks, spans = spread_chunks(arrived, part, small_part)
+
+    cond_vec = pooled.astype(jnp.float32) + embedding(timestep, layer_width)
+    activated = jax.nn.silu(cond_vec).astype(jnp.bfloat16)
+    by_block = activated.reshape(pooled.shape[0], count_f, -1).transpose(1, 0, 2)
+    pieces = [pick(by_block, fsdp_index)]
+    for step in range(1, count_f):
+        pieces.append(shift(pick(by_block, (fsdp_index + step) % count_f), step))
+    per_pair = pooled.shape[0]
+    if not dense:
+        late = [at for at, (step, mask, *_) in enumerate(spans) if (step, mask) == (count_f - 2, 2)]
+        pieces = lax.optimization_barrier((pieces, chunks[late[0]] if late else arrived[-1]))[0]
+    partial_value = jnp.dot(
+        jnp.concatenate(pieces, axis=0), modulation_weight, preferred_element_type=jnp.float32
+    )
+    own_part = partial_value[:per_pair]
+    for step in range(1, count_f):
+        own_part = own_part + shift(
+            partial_value[per_pair * step : per_pair * (step + 1)], count_f - step
+        )
+    mod_plane = [own_part] + [swap(own_part, 2 * mask) for mask in range(1, count_s // 2)]
+    mod_pieces = []
+    for piece in mod_plane:
+        mod_pieces += [piece, swap(piece, 1)]
+
     tokens = 2 * tok_seq
     inputs = (
         policy_attention.reshape(tokens, feature_index),
@@ -527,8 +540,7 @@
         small_weights,
         *mod_pieces,
     )
-    part, small_part = feature_index // count_s, small_weights.shape[0] // count_s
-    if down_block % 128 or block % 128 or part % 16 or small_part % 16 or rank % 32:
+    if dense:
         keep, send, dstream, attn = dense_step(
             fsdp_index,
             seq_index,
@@ -545,9 +557,9 @@
         )
     else:
         keep, send, dstream, attn = step_call(
-            jnp.stack([fsdp_index, seq_index]).astype(jnp.int32),
             inputs,
-            *gather_chunks(frozen_output_weight, small_weights, seq_index),
+            chunks,
+            spans,
             tokens,
             feature_index,
             layer_width,
@@ -571,9 +583,8 @@
     pair_sum = (weight_pair * total[:, :, :width]).astype(jnp.bfloat16)
     own_sum = pick(pair_sum, fsdp_index).astype(jnp.float32)
     for step in range(1, count_f):
-        own_sum = own_sum + shift(pick(pair_sum, (fsdp_index + step) % count_f), step).astype(
-            jnp.float32
-        )
+        arrived_sum = shift(pick(pair_sum, (fsdp_index + step) % count_f), step)
+        own_sum = own_sum + arrived_sum.astype(jnp.float32)
     gathered = gather_seq(own_sum.astype(jnp.bfloat16), seq_index)
     gathered = gathered.reshape(plane_count, 2, rank // count_s, width).transpose(1, 0, 2, 3)
     sums = gathered.reshape(rank, width).astype(jnp.float32)

time: 159 us -> 166 us (1.044)
  waiting for transfers between devices: 64.3 us -> 71.4 us
    ppermute x15, waiting for transfers between devices: 18.2 us -> 29.1 us  [shift(): lax.ppermute(value, 'fsdp', [(i, (i + step) % count) for i in range(count)])]
    ppermute x15, starting transfers between devices: 29.3 us -> 36.2 us  [shift(): lax.ppermute(value, 'fsdp', [(i, (i + step) % count) for i in range(count)])]
    ppermute x42, starting transfers between devices: 30.5 us -> 25 us  [swap(): return lax.ppermute(value, 'seq', [(i, i ^ mask) for i in range(count)])]
    ppermute x42, waiting for transfers between devices: 46.1 us -> 42.2 us  [swap(): return lax.ppermute(value, 'seq', [(i, i ^ mask) for i in range(count)])]
  transfers between devices with their start and end apart: 57 -> 57, of which waited for: 32 -> 32; matrix products, arithmetic and copies ran while one was open for 4% -> 2% of each run, Pallas kernels for 0% -> 0%
where the time goes in v1:
time: 166 us; the launch traced here: 165 us
  waiting for transfers between devices  71.4 us (43%)
  starting transfers between devices  61.1 us (37%)
  Pallas kernels  14.4 us (9%)
  other arithmetic  8.05 us (5%)
  local copies, waits for them, and re-layouts  5.33 us (3%)
  between operations  4.62 us (3%)
    ppermute x42, waiting for transfers between devices, swap(): return lax.ppermute(value, 'seq', [(i, i ^ mask) for i in range(count)])  42.2 us
    ppermute x15, starting transfers between devices, shift(): lax.ppermute(value, 'fsdp', [(i, (i + step) % count) for i in range(count)])  36.2 us
    ppermute x15, waiting for transfers between devices, shift(): lax.ppermute(value, 'fsdp', [(i, (i + step) % count) for i in range(count)])  29.1 us
    ppermute x42, starting transfers between devices, swap(): return lax.ppermute(value, 'seq', [(i, i ^ mask) for i in range(count)])  25 us
    pallas_call x1, Pallas kernels, step_call(): pl.pallas_call(lambda *refs: step_kernel(sizes, *refs), out_shape=(grads,...  14.4 us
  transfers between devices with their start and end apart: 57, of which 32 were waited for; matrix products, arithmetic and copies ran while one was open for 2% of the time, Pallas kernels for 0%

profile of v1, /device:TPU:0, one launch (start us, length us, event | category | flops | bytes accessed | tf_op | source)
XLA Modules:
  0.0 165.3 jit_solution(17051986409295242966)
XLA Ops:
  3.0 4.1 %collective-permute-start.3 = (bf16[224,768]{1,0:T(8,128)(2,1)S(1)}, bf16[224,768]{1,0:T(8,128)(2,1)}, u32[]{:S(2)}, u32[]{:S(2)}) collective-permute-start(bf16[224,768]{1,0:T(8,128)(2,1)S(1)} %pad_maximum_fusion), channel_id=1, source_target_pairs={{0,16},{8,24},{16,0},{24,8},{1,17},{9,25},{17,1},{25,9},{2,18},{10... | collective-permute-start | bytes 1032200 | tf_op jit(solution)/shard_map/ppermute | solution.py:35
  8.7 2.2 %collective-permute-start.33 = (bf16[224,768]{1,0:T(8,128)(2,1)S(1)}, bf16[224,768]{1,0:T(8,128)(2,1)}, u32[]{:S(2)}, u32[]{:S(2)}) collective-permute-start(bf16[224,768]{1,0:T(8,128)(2,1)S(1)} %pad_maximum_fusion), channel_id=1, source_target_pairs={{0,24},{8,0},{16,8},{24,16},{1,25},{9,1},{17,9},{25,17},{2,26},{10... | collective-permute-start | bytes 1032200 | tf_op jit(solution)/shard_map/ppermute | solution.py:35
  11.6 19.3 %collective-permute-done.3.refs_26_ = bf16[224,768]{1,0:T(8,128)(2,1)} collective-permute-done((bf16[224,768]{1,0:T(8,128)(2,1)S(1)}, bf16[224,768]{1,0:T(8,128)(2,1)}, u32[]{:S(2)}, u32[]{:S(2)}) %collective-permute-start.3) | collective-permute-done | bytes 344096 | tf_op jit(solution)/shard_map/ppermute | solution.py:35
  33.4 1.8 %collective-permute-start.19 = (bf16[224,768]{1,0:T(8,128)(2,1)}, bf16[224,768]{1,0:T(8,128)(2,1)S(1)}, u32[]{:S(2)}, u32[]{:S(2)}) collective-permute-start(bf16[224,768]{1,0:T(8,128)(2,1)} %collective-permute-done.15.refs_16_), channel_id=1, source_target_pairs={{0,4},{1,5},{2,6},{3,7},{4,0},{5,1},{6,2},{7,3},{8,12},{9,13},{10,... | collective-permute-start | bytes 1032200 | tf_op jit(solution)/shard_map/ppermute | solution.py:40
  35.3 5.9 %collective-permute-start = (bf16[1,768]{1,0:T(2,128)(2,1)S(1)}, bf16[1,768]{1,0:T(2,128)(2,1)S(1)}, u32[]{:S(2)}, u32[]{:S(2)}) collective-permute-start(bf16[1,768]{1,0:T(2,128)(2,1)S(1)} %get-tuple-element.37), channel_id=1, source_target_pairs={{0,8},{8,16},{16,24},{24,0},{1,9},{9,17},{17,25},{25,1},{2,10},{10... | collective-permute-start | bytes 4616 | tf_op jit(solution)/shard_map/ppermute | solution.py:35
  42.5 4.3 %collective-permute-start.1 = (bf16[1,768]{1,0:T(2,128)(2,1)S(1)}, bf16[1,768]{1,0:T(2,128)(2,1)S(1)}, u32[]{:S(2)}, u32[]{:S(2)}) collective-permute-start(bf16[1,768]{1,0:T(2,128)(2,1)S(1)} %get-tuple-element.36), channel_id=1, source_target_pairs={{0,16},{8,24},{16,0},{24,8},{1,17},{9,25},{17,1},{25,9},{2,18},{10... | collective-permute-start | bytes 4616 | tf_op jit(solution)/shard_map/ppermute | solution.py:35
  48.3 2.4 %collective-permute-start.2 = (bf16[1,768]{1,0:T(2,128)(2,1)S(1)}, bf16[1,768]{1,0:T(2,128)(2,1)S(1)}, u32[]{:S(2)}, u32[]{:S(2)}) collective-permute-start(bf16[1,768]{1,0:T(2,128)(2,1)S(1)} %get-tuple-element.35), channel_id=1, source_target_pairs={{0,24},{8,0},{16,8},{24,16},{1,25},{9,1},{17,9},{25,17},{2,26},{10... | collective-permute-start | bytes 4616 | tf_op jit(solution)/shard_map/ppermute | solution.py:35
  55.5 7.0 %collective-permute-done.27.refs_30_ = bf16[224,768]{1,0:T(8,128)(2,1)S(1)} collective-permute-done((bf16[224,768]{1,0:T(8,128)(2,1)}, bf16[224,768]{1,0:T(8,128)(2,1)S(1)}, u32[]{:S(2)}, u32[]{:S(2)}) %collective-permute-start.27) | collective-permute-done | bytes 344096 | tf_op jit(solution)/shard_map/ppermute | solution.py:40
  62.6 3.8 %collective-permute-start.5 = (f32[1,1152]{1,0:T(1,128)S(1)}, f32[1,1152]{1,0:T(1,128)S(1)}, u32[]{:S(2)}, u32[]{:S(2)}) collective-permute-start(f32[1,1152]{1,0:T(1,128)S(1)} %get-tuple-element.32), channel_id=1, source_target_pairs={{0,24},{8,0},{16,8},{24,16},{1,25},{9,1},{17,9},{25,17},{2,26},{10... | collective-permute-start | bytes 13832 | tf_op jit(solution)/shard_map/ppermute | solution.py:35
  74.0 5.8 %collective-permute-done.9.refs_10_ = f32[1,1152]{1,0:T(1,128)S(1)} collective-permute-done((f32[1,1152]{1,0:T(1,128)S(1)}, f32[1,1152]{1,0:T(1,128)S(1)}, u32[]{:S(2)}, u32[]{:S(2)}) %collective-permute-start.9) | collective-permute-done | bytes 4640 | tf_op jit(solution)/shard_map/ppermute | solution.py:40
  80.6 2.8 %collective-permute-done.11.refs_12_ = f32[1,1152]{1,0:T(1,128)S(1)} collective-permute-done((f32[1,1152]{1,0:T(1,128)S(1)}, f32[1,1152]{1,0:T(1,128)S(1)}, u32[]{:S(2)}, u32[]{:S(2)}) %collective-permute-start.11) | collective-permute-done | bytes 4640 | tf_op jit(solution)/shard_map/ppermute | solution.py:40
  83.9 4.0 %collective-permute-done.13.refs_14_ = f32[1,1152]{1,0:T(1,128)S(1)} collective-permute-done((f32[1,1152]{1,0:T(1,128)S(1)}, f32[1,1152]{1,0:T(1,128)S(1)}, u32[]{:S(2)}, u32[]{:S(2)}) %collective-permute-start.13) | collective-permute-done | bytes 4640 | tf_op jit(solution)/shard_map/ppermute | solution.py:40
  94.3 4.7 %collective-permute-done.39.refs_42_ = bf16[112,768]{1,0:T(8,128)(2,1)S(1)} collective-permute-done((bf16[112,768]{1,0:T(8,128)(2,1)S(1)}, bf16[112,768]{1,0:T(8,128)(2,1)S(1)}, u32[]{:S(2)}, u32[]{:S(2)}) %collective-permute-start.39) | collective-permute-done | bytes 172064 | tf_op jit(solution)/shard_map/ppermute | solution.py:40
  105.0 14.4 %step.1 = (bf16[4,32,2048]{2,1,0:T(8,128)(2,1)}, bf16[4,32,2048]{2,1,0:T(8,128)(2,1)}, f32[128,3072]{1,0:T(8,128)}, f32[128,1536]{1,0:T(8,128)}) custom-call(bf16[128,1536]{1,0:T(8,128)(2,1)} %bitcast.59, bf16[128,1536]{1,0:T(8,128)(2,1)} %bitcast.60, bf16[128,3072]{1,0:T(8,128)(2,1)} %bitcast.56, bf16[128,3072]{1,0:T(8,128)(2,1)} %bitcast.57, ...), custom_call_target="tpu_custom_call" | custom-call | tf_op jit(solution)/shard_map/step/pallas_call | solution.py:302
  119.6 2.0 %collective-permute-done.43 = bf16[4,32,2048]{2,1,0:T(8,128)(2,1)S(1)} collective-permute-done((bf16[4,32,2048]{2,1,0:T(8,128)(2,1)}, bf16[4,32,2048]{2,1,0:T(8,128)(2,1)S(1)}, u32[]{:S(2)}, u32[]{:S(2)}) %collective-permute-start.43) | collective-permute-done | bytes 524320 | tf_op jit(solution)/shard_map/ppermute | solution.py:40
  124.5 1.9 %collective-permute-start.46 = (bf16[4,8,2048]{2,1,0:T(8,128)(2,1)S(1)}, bf16[4,8,2048]{2,1,0:T(8,128)(2,1)S(1)}, u32[]{:S(2)}, u32[]{:S(2)}) collective-permute-start(bf16[4,8,2048]{2,1,0:T(8,128)(2,1)S(1)} %get-tuple-element.25), channel_id=1, source_target_pairs={{0,6},{1,7},{2,4},{3,5},{4,2},{5,3},{6,0},{7,1},{8,14},{9,15},{10,... | collective-permute-start | bytes 393224 | tf_op jit(solution)/shard_map/ppermute | solution.py:40
  126.4 2.9 %collective-permute-done.44 = bf16[4,8,2048]{2,1,0:T(8,128)(2,1)S(1)} collective-permute-done((bf16[4,8,2048]{2,1,0:T(8,128)(2,1)S(1)}, bf16[4,8,2048]{2,1,0:T(8,128)(2,1)S(1)}, u32[]{:S(2)}, u32[]{:S(2)}) %collective-permute-start.44) | collective-permute-done | bytes 131104 | tf_op jit(solution)/shard_map/ppermute | solution.py:40
  129.3 2.7 %collective-permute-done.46 = bf16[4,8,2048]{2,1,0:T(8,128)(2,1)S(1)} collective-permute-done((bf16[4,8,2048]{2,1,0:T(8,128)(2,1)S(1)}, bf16[4,8,2048]{2,1,0:T(8,128)(2,1)S(1)}, u32[]{:S(2)}, u32[]{:S(2)}) %collective-permute-start.46) | collective-permute-done | bytes 131104 | tf_op jit(solution)/shard_map/ppermute | solution.py:40
  133.4 2.4 %collective-permute-start.47 = (bf16[8,1920]{1,0:T(8,128)(2,1)S(1)}, bf16[8,1920]{1,0:T(8,128)(2,1)S(1)}, u32[]{:S(2)}, u32[]{:S(2)}) collective-permute-start(bf16[8,1920]{1,0:T(8,128)(2,1)S(1)} %get-tuple-element.29), channel_id=1, source_target_pairs={{0,8},{8,16},{16,24},{24,0},{1,9},{9,17},{17,25},{25,1},{2,10},{10... | collective-permute-start | bytes 92168 | tf_op jit(solution)/shard_map/ppermute | solution.py:35
  136.7 2.7 %collective-permute-start.49 = (bf16[8,1920]{1,0:T(8,128)(2,1)S(1)}, bf16[8,1920]{1,0:T(8,128)(2,1)S(1)}, u32[]{:S(2)}, u32[]{:S(2)}) collective-permute-start(bf16[8,1920]{1,0:T(8,128)(2,1)S(1)} %get-tuple-element.30), channel_id=1, source_target_pairs={{0,24},{8,0},{16,8},{24,16},{1,25},{9,1},{17,9},{25,17},{2,26},{10... | collective-permute-start | bytes 92168 | tf_op jit(solution)/shard_map/ppermute | solution.py:35
  146.1 2.1 %collective-permute-done.52 = bf16[8,1920]{1,0:T(8,128)(2,1)S(1)} collective-permute-done((bf16[8,1920]{1,0:T(8,128)(2,1)S(1)}, bf16[8,1920]{1,0:T(8,128)(2,1)S(1)}, u32[]{:S(2)}, u32[]{:S(2)}) %collective-permute-start.52) | collective-permute-done | bytes 30752 | tf_op jit(solution)/shard_map/ppermute | solution.py:40
  148.3 2.5 %multiply_convert_fusion = bf16[128,3072]{1,0:T(8,128)(2,1)} fusion(f32[128,3072]{1,0:T(8,128)} %get-tuple-element.20, f32[]{:T(128)S(6)} %div.30), kind=kLoop, calls=%fused_computation | loop fusion | flops 786432 | bytes 2359300 | tf_op jit(solution)/shard_map/convert_element_type | solution.py:581
  153.5 3.6 %collective-permute-start.55 = (f32[8,128]{1,0:T(8,128)S(1)}, f32[8,128]{1,0:T(8,128)S(1)}, u32[]{:S(2)}, u32[]{:S(2)}) collective-permute-start(f32[8,128]{1,0:T(8,128)S(1)} %broadcast_in_dim.2), channel_id=1, source_target_pairs={{0,16},{8,24},{16,0},{24,8},{1,17},{9,25},{17,1},{25,9},{2,18},{10... | collective-permute-start | bytes 12296 | tf_op jit(solution)/shard_map/ppermute | solution.py:35
  158.8 2.0 %collective-permute-done.56 = f32[8,128]{1,0:T(8,128)S(1)} collective-permute-done((f32[8,128]{1,0:T(8,128)S(1)}, f32[8,128]{1,0:T(8,128)S(1)}, u32[]{:S(2)}, u32[]{:S(2)}) %collective-permute-start.56) | collective-permute-done | bytes 4128 | tf_op jit(solution)/shard_map/ppermute | solution.py:35
  (219 shorter events, 53.3 us)
Async XLA Ops:
  3.0 27.9 %collective-permute-start.3 = (bf16[224,768]{1,0:T(8,128)(2,1)S(1)}, bf16[224,768]{1,0:T(8,128)(2,1)}, u32[]{:S(2)}, u32[]{:S(2)}) collective-permute-start(bf16[224,768]{1,0:T(8,128)(2,1)S(1)} %pad_maximum_fusion), channel_id=1, source_target_pairs={{0,16},{8,24},{16,0},{24,8},{1,17},{9,25},{17,1},{25,9},{2,18},{10... | collective-permute-start | bytes 1032200 | tf_op jit(solution)/shard_map/ppermute | solution.py:35
  7.1 26.0 %collective-permute-start.15 = (bf16[224,768]{1,0:T(8,128)(2,1)S(1)}, bf16[224,768]{1,0:T(8,128)(2,1)}, u32[]{:S(2)}, u32[]{:S(2)}) collective-permute-start(bf16[224,768]{1,0:T(8,128)(2,1)S(1)} %pad_maximum_fusion), channel_id=1, source_target_pairs={{0,8},{8,16},{16,24},{24,0},{1,9},{9,17},{17,25},{25,1},{2,10},{10... | collective-permute-start | bytes 1032200 | tf_op jit(solution)/shard_map/ppermute | solution.py:35
  8.7 43.8 %collective-permute-start.33 = (bf16[224,768]{1,0:T(8,128)(2,1)S(1)}, bf16[224,768]{1,0:T(8,128)(2,1)}, u32[]{:S(2)}, u32[]{:S(2)}) collective-permute-start(bf16[224,768]{1,0:T(8,128)(2,1)S(1)} %pad_maximum_fusion), channel_id=1, source_target_pairs={{0,24},{8,0},{16,8},{24,16},{1,25},{9,1},{17,9},{25,17},{2,26},{10... | collective-permute-start | bytes 1032200 | tf_op jit(solution)/shard_map/ppermute | solution.py:35
  31.0 22.1 %collective-permute-start.4 = (bf16[224,768]{1,0:T(8,128)(2,1)}, bf16[224,768]{1,0:T(8,128)(2,1)S(1)}, u32[]{:S(2)}, u32[]{:S(2)}) collective-permute-start(bf16[224,768]{1,0:T(8,128)(2,1)} %collective-permute-done.3.refs_26_), channel_id=1, source_target_pairs={{0,2},{1,3},{2,0},{3,1},{4,6},{5,7},{6,4},{7,5},{8,10},{9,11},{10,... | collective-permute-start | bytes 1032200 | tf_op jit(solution)/shard_map/ppermute | solution.py:40
  33.1 21.8 %collective-permute-start.17 = (bf16[224,768]{1,0:T(8,128)(2,1)}, bf16[224,768]{1,0:T(8,128)(2,1)S(1)}, u32[]{:S(2)}, u32[]{:S(2)}) collective-permute-start(bf16[224,768]{1,0:T(8,128)(2,1)} %collective-permute-done.15.refs_16_), channel_id=1, source_target_pairs={{0,2},{1,3},{2,0},{3,1},{4,6},{5,7},{6,4},{7,5},{8,10},{9,11},{10,... | collective-permute-start | bytes 1032200 | tf_op jit(solution)/shard_map/ppermute | solution.py:40
  33.4 21.6 %collective-permute-start.19 = (bf16[224,768]{1,0:T(8,128)(2,1)}, bf16[224,768]{1,0:T(8,128)(2,1)S(1)}, u32[]{:S(2)}, u32[]{:S(2)}) collective-permute-start(bf16[224,768]{1,0:T(8,128)(2,1)} %collective-permute-done.15.refs_16_), channel_id=1, source_target_pairs={{0,4},{1,5},{2,6},{3,7},{4,0},{5,1},{6,2},{7,3},{8,12},{9,13},{10,... | collective-permute-start | bytes 1032200 | tf_op jit(solution)/shard_map/ppermute | solution.py:40
  35.3 7.2 %collective-permute-start = (bf16[1,768]{1,0:T(2,128)(2,1)S(1)}, bf16[1,768]{1,0:T(2,128)(2,1)S(1)}, u32[]{:S(2)}, u32[]{:S(2)}) collective-permute-start(bf16[1,768]{1,0:T(2,128)(2,1)S(1)} %get-tuple-element.37), channel_id=1, source_target_pairs={{0,8},{8,16},{16,24},{24,0},{1,9},{9,17},{17,25},{25,1},{2,10},{10... | collective-permute-start | bytes 4616 | tf_op jit(solution)/shard_map/ppermute | solution.py:35
  52.0 10.6 %collective-permute-start.27 = (bf16[224,768]{1,0:T(8,128)(2,1)}, bf16[224,768]{1,0:T(8,128)(2,1)S(1)}, u32[]{:S(2)}, u32[]{:S(2)}) collective-permute-start(bf16[224,768]{1,0:T(8,128)(2,1)} %collective-permute-done.3.refs_26_), channel_id=1, source_target_pairs={{0,4},{1,5},{2,6},{3,7},{4,0},{5,1},{6,2},{7,3},{8,12},{9,13},{10,... | collective-permute-start | bytes 1032200 | tf_op jit(solution)/shard_map/ppermute | solution.py:40
  52.5 13.8 %collective-permute-start.35 = (bf16[224,768]{1,0:T(8,128)(2,1)}, bf16[224,768]{1,0:T(8,128)(2,1)S(1)}, u32[]{:S(2)}, u32[]{:S(2)}) collective-permute-start(bf16[224,768]{1,0:T(8,128)(2,1)} %collective-permute-done.33.refs_36_), channel_id=1, source_target_pairs={{0,2},{1,3},{2,0},{3,1},{4,6},{5,7},{6,4},{7,5},{8,10},{9,11},{10,... | collective-permute-start | bytes 1032200 | tf_op jit(solution)/shard_map/ppermute | solution.py:40
  53.1 13.3 %collective-permute-start.37 = (bf16[224,768]{1,0:T(8,128)(2,1)}, bf16[224,768]{1,0:T(8,128)(2,1)S(1)}, u32[]{:S(2)}, u32[]{:S(2)}) collective-permute-start(bf16[224,768]{1,0:T(8,128)(2,1)} %collective-permute-done.33.refs_36_), channel_id=1, source_target_pairs={{0,4},{1,5},{2,6},{3,7},{4,0},{5,1},{6,2},{7,3},{8,12},{9,13},{10,... | collective-permute-start | bytes 1032200 | tf_op jit(solution)/shard_map/ppermute | solution.py:40
  54.9 12.7 %collective-permute-start.16 = (bf16[224,768]{1,0:T(8,128)(2,1)}, bf16[224,768]{1,0:T(8,128)(2,1)S(1)}, u32[]{:S(2)}, u32[]{:S(2)}) collective-permute-start(bf16[224,768]{1,0:T(8,128)(2,1)} %collective-permute-done.15.refs_16_), channel_id=1, source_target_pairs={{0,1},{1,0},{2,3},{3,2},{4,5},{5,4},{6,7},{7,6},{8,9},{9,8},{10,11... | collective-permute-start | bytes 1032200 | tf_op jit(solution)/shard_map/ppermute | solution.py:40
  55.0 12.7 %collective-permute-start.25 = (bf16[224,768]{1,0:T(8,128)(2,1)}, bf16[224,768]{1,0:T(8,128)(2,1)S(1)}, u32[]{:S(2)}, u32[]{:S(2)}) collective-permute-start(bf16[224,768]{1,0:T(8,128)(2,1)} %collective-permute-done.3.refs_26_), channel_id=1, source_target_pairs={{0,1},{1,0},{2,3},{3,2},{4,5},{5,4},{6,7},{7,6},{8,9},{9,8},{10,11... | collective-permute-start | bytes 1032200 | tf_op jit(solution)/shard_map/ppermute | solution.py:40
  67.7 25.6 %collective-permute-start.29 = (bf16[112,768]{1,0:T(8,128)(2,1)S(1)}, bf16[112,768]{1,0:T(8,128)(2,1)S(1)}, u32[]{:S(2)}, u32[]{:S(2)}) collective-permute-start(bf16[112,768]{1,0:T(8,128)(2,1)S(1)} %slice.86), channel_id=1, source_target_pairs={{0,4},{1,5},{2,6},{3,7},{4,0},{5,1},{6,2},{7,3},{8,12},{9,13},{10,... | collective-permute-start | bytes 516104 | tf_op jit(solution)/shard_map/ppermute | solution.py:40
  68.6 25.1 %collective-permute-start.21 = (bf16[112,768]{1,0:T(8,128)(2,1)S(1)}, bf16[112,768]{1,0:T(8,128)(2,1)S(1)}, u32[]{:S(2)}, u32[]{:S(2)}) collective-permute-start(bf16[112,768]{1,0:T(8,128)(2,1)S(1)} %slice.84), channel_id=1, source_target_pairs={{0,4},{1,5},{2,6},{3,7},{4,0},{5,1},{6,2},{7,3},{8,12},{9,13},{10,... | collective-permute-start | bytes 516104 | tf_op jit(solution)/shard_map/ppermute | solution.py:40
  70.9 22.8 %collective-permute-start.23 = (bf16[112,768]{1,0:T(8,128)(2,1)S(1)}, bf16[112,768]{1,0:T(8,128)(2,1)S(1)}, u32[]{:S(2)}, u32[]{:S(2)}) collective-permute-start(bf16[112,768]{1,0:T(8,128)(2,1)S(1)} %slice.85), channel_id=1, source_target_pairs={{0,2},{1,3},{2,0},{3,1},{4,6},{5,7},{6,4},{7,5},{8,10},{9,11},{10,... | collective-permute-start | bytes 516104 | tf_op jit(solution)/shard_map/ppermute | solution.py:40
  71.8 22.3 %collective-permute-start.31 = (bf16[112,768]{1,0:T(8,128)(2,1)S(1)}, bf16[112,768]{1,0:T(8,128)(2,1)S(1)}, u32[]{:S(2)}, u32[]{:S(2)}) collective-permute-start(bf16[112,768]{1,0:T(8,128)(2,1)S(1)} %slice.87), channel_id=1, source_target_pairs={{0,2},{1,3},{2,0},{3,1},{4,6},{5,7},{6,4},{7,5},{8,10},{9,11},{10,... | collective-permute-start | bytes 516104 | tf_op jit(solution)/shard_map/ppermute | solution.py:40
  72.9 6.8 %collective-permute-start.9 = (f32[1,1152]{1,0:T(1,128)S(1)}, f32[1,1152]{1,0:T(1,128)S(1)}, u32[]{:S(2)}, u32[]{:S(2)}) collective-permute-start(f32[1,1152]{1,0:T(1,128)S(1)} %fusion.19.refs_8_), channel_id=1, source_target_pairs={{0,2},{1,3},{2,0},{3,1},{4,6},{5,7},{6,4},{7,5},{8,10},{9,11},{10,... | collective-permute-start | bytes 13832 | tf_op jit(solution)/shard_map/ppermute | solution.py:40
  92.6 6.4 %collective-permute-start.39 = (bf16[112,768]{1,0:T(8,128)(2,1)S(1)}, bf16[112,768]{1,0:T(8,128)(2,1)S(1)}, u32[]{:S(2)}, u32[]{:S(2)}) collective-permute-start(bf16[112,768]{1,0:T(8,128)(2,1)S(1)} %slice.88), channel_id=1, source_target_pairs={{0,4},{1,5},{2,6},{3,7},{4,0},{5,1},{6,2},{7,3},{8,12},{9,13},{10,... | collective-permute-start | bytes 516104 | tf_op jit(solution)/shard_map/ppermute | solution.py:40
  93.4 6.2 %collective-permute-start.41 = (bf16[112,768]{1,0:T(8,128)(2,1)S(1)}, bf16[112,768]{1,0:T(8,128)(2,1)S(1)}, u32[]{:S(2)}, u32[]{:S(2)}) collective-permute-start(bf16[112,768]{1,0:T(8,128)(2,1)S(1)} %slice.89), channel_id=1, source_target_pairs={{0,2},{1,3},{2,0},{3,1},{4,6},{5,7},{6,4},{7,5},{8,10},{9,11},{10,... | collective-permute-start | bytes 516104 | tf_op jit(solution)/shard_map/ppermute | solution.py:40
  93.7 6.4 %collective-permute-start.22 = (bf16[112,768]{1,0:T(8,128)(2,1)S(1)}, bf16[112,768]{1,0:T(8,128)(2,1)S(1)}, u32[]{:S(2)}, u32[]{:S(2)}) collective-permute-start(bf16[112,768]{1,0:T(8,128)(2,1)S(1)} %collective-permute-done.21.refs_22_), channel_id=1, source_target_pairs={{0,1},{1,0},{2,3},{3,2},{4,5},{5,4},{6,7},{7,6},{8,9},{9,8},{10,11... | collective-permute-start | bytes 516104 | tf_op jit(solution)/shard_map/ppermute | solution.py:40
  94.2 7.8 %collective-permute-start.26 = (bf16[224,768]{1,0:T(8,128)(2,1)S(1)}, bf16[224,768]{1,0:T(8,128)(2,1)S(1)}, u32[]{:S(2)}, u32[]{:S(2)}) collective-permute-start(bf16[224,768]{1,0:T(8,128)(2,1)S(1)} %collective-permute-done.4.refs_28_), channel_id=1, source_target_pairs={{0,1},{1,0},{2,3},{3,2},{4,5},{5,4},{6,7},{7,6},{8,9},{9,8},{10,11... | collective-permute-start | bytes 1032200 | tf_op jit(solution)/shard_map/ppermute | solution.py:40
  122.8 6.4 %collective-permute-start.44 = (bf16[4,8,2048]{2,1,0:T(8,128)(2,1)S(1)}, bf16[4,8,2048]{2,1,0:T(8,128)(2,1)S(1)}, u32[]{:S(2)}, u32[]{:S(2)}) collective-permute-start(bf16[4,8,2048]{2,1,0:T(8,128)(2,1)S(1)} %get-tuple-element.24), channel_id=1, source_target_pairs={{0,2},{1,3},{2,0},{3,1},{4,6},{5,7},{6,4},{7,5},{8,10},{9,11},{10,... | collective-permute-start | bytes 393224 | tf_op jit(solution)/shard_map/ppermute | solution.py:40
  124.5 7.4 %collective-permute-start.46 = (bf16[4,8,2048]{2,1,0:T(8,128)(2,1)S(1)}, bf16[4,8,2048]{2,1,0:T(8,128)(2,1)S(1)}, u32[]{:S(2)}, u32[]{:S(2)}) collective-permute-start(bf16[4,8,2048]{2,1,0:T(8,128)(2,1)S(1)} %get-tuple-element.25), channel_id=1, source_target_pairs={{0,6},{1,7},{2,4},{3,5},{4,2},{5,3},{6,0},{7,1},{8,14},{9,15},{10,... | collective-permute-start | bytes 393224 | tf_op jit(solution)/shard_map/ppermute | solution.py:40
  133.4 6.1 %collective-permute-start.47 = (bf16[8,1920]{1,0:T(8,128)(2,1)S(1)}, bf16[8,1920]{1,0:T(8,128)(2,1)S(1)}, u32[]{:S(2)}, u32[]{:S(2)}) collective-permute-start(bf16[8,1920]{1,0:T(8,128)(2,1)S(1)} %get-tuple-element.29), channel_id=1, source_target_pairs={{0,8},{8,16},{16,24},{24,0},{1,9},{9,17},{17,25},{25,1},{2,10},{10... | collective-permute-start | bytes 92168 | tf_op jit(solution)/shard_map/ppermute | solution.py:35
  (72 other events, 838.6 us)

commit v2 on v1

--- a/solution.py
+++ b/solution.py
@@ -173,7 +173,7 @@
         late.append(start(mod_pieces[mask], mod_hold.at[place], slot + mask))
     for copy in first:
         copy.wait()
-    for step in range(count_f):
+    for step in [0] + shift_order(count_f):
         for copy in blocks[step]:
             copy.wait()
         at = lax.rem(fsdp_index - step + count_f, count_f)
@@ -329,6 +329,10 @@
     )(*operands, *chunks)
 
 
+def shift_order(count_f):
+    return sorted(range(1, count_f), key=lambda step: step * (count_f - step))
+
+
 def send_chunks(own, own_small, seq_index):
     count_f, count_s = lax.axis_size("fsdp"), lax.axis_size("seq")
     part, small_part = own.shape[0] // count_s, own_small.shape[0] // count_s
@@ -341,7 +345,7 @@
         axis=0,
     )
     arrived = []
-    for step in range(1, count_f):
+    for step in shift_order(count_f):
         arrived.append(shift(chunk, step))
     return arrived
 
@@ -351,24 +355,24 @@
     middle = (part + small_part) // 32 * 16
     chunks, spans = [], []
 
-    def add(step, mask, first_row, piece):
+    def add(mask, first_row, piece):
         chunks.extend([piece, swap(piece, 1)])
         spans.append((step, mask, first_row, piece.shape[0]))
         spans.append((step, mask + 1, first_row, piece.shape[0]))
 
-    for step in range(1, count_f):
-        held = arrived[step - 1]
-        add(step, 0, 0, held)
+    for number, step in enumerate(shift_order(count_f), 1):
+        held = arrived[number - 1]
+        add(0, 0, held)
         if count_s == 8:
             first, second = swap(held, 2), swap(held, 4)
             top, bottom = swap(first[:middle], 4), swap(second[middle:], 2)
-            add(step, 2, 0, first)
-            add(step, 4, 0, second)
-            add(step, 6, 0, top)
-            add(step, 6, middle, bottom)
+            add(2, 0, first)
+            add(4, 0, second)
+            add(6, 0, top)
+            add(6, middle, bottom)
         else:
             for mask in range(2, count_s, 2):
-                add(step, mask, 0, swap(held, mask))
+                add(mask, 0, swap(held, mask))
     return chunks, tuple(spans)
 
 
@@ -513,8 +517,8 @@
         pieces.append(shift(pick(by_block, (fsdp_index + step) % count_f), step))
     per_pair = pooled.shape[0]
     if not dense:
-        late = [at for at, (step, mask, *_) in enumerate(spans) if (step, mask) == (count_f - 2, 2)]
-        pieces = lax.optimization_barrier((pieces, chunks[late[0]] if late else arrived[-1]))[0]
+        late = [at for at, (step, mask, *_) in enumerate(spans) if (step, mask) == (1, 2)]
+        pieces = lax.optimization_barrier((pieces, chunks[late[0]] if late else arrived[0]))[0]
     partial_value = jnp.dot(
         jnp.concatenate(pieces, axis=0), modulation_weight, preferred_element_type=jnp.float32
     )

time: 166 us -> 157 us (0.946)
  waiting for transfers between devices: 71.4 us -> 57.4 us
  starting transfers between devices: 61.1 us -> 66.2 us
    ppermute x15, waiting for transfers between devices: 29.1 us -> 18.4 us  [shift(): lax.ppermute(value, 'fsdp', [(i, (i + step) % count) for i in range(count)])]
    ppermute x42, starting transfers between devices: 25 us -> 29.2 us  [swap(): return lax.ppermute(value, 'seq', [(i, i ^ mask) for i in range(count)])]
    ppermute x42, waiting for transfers between devices: 42.2 us -> 39.1 us  [swap(): return lax.ppermute(value, 'seq', [(i, i ^ mask) for i in range(count)])]
  transfers between devices with their start and end apart: 57 -> 57, of which waited for: 32 -> 33; matrix products, arithmetic and copies ran while one was open for 2% -> 3% of each run, Pallas kernels for 0% -> 0%
where the time goes in v2:
time: 157 us; the launch traced here: 156 us
  starting transfers between devices  66.2 us (42%)
  waiting for transfers between devices  57.4 us (37%)
  Pallas kernels  14.4 us (9%)
  other arithmetic  8.05 us (5%)
  local copies, waits for them, and re-layouts  5.41 us (3%)
  between operations  4.59 us (3%)
    ppermute x42, waiting for transfers between devices, swap(): return lax.ppermute(value, 'seq', [(i, i ^ mask) for i in range(count)])  39.1 us
    ppermute x15, starting transfers between devices, shift(): lax.ppermute(value, 'fsdp', [(i, (i + step) % count) for i in range(count)])  37.1 us
    ppermute x42, starting transfers between devices, swap(): return lax.ppermute(value, 'seq', [(i, i ^ mask) for i in range(count)])  29.2 us
    ppermute x15, waiting for transfers between devices, shift(): lax.ppermute(value, 'fsdp', [(i, (i + step) % count) for i in range(count)])  18.4 us
    pallas_call x1, Pallas kernels, step_call(): pl.pallas_call(lambda *refs: step_kernel(sizes, *refs), out_shape=(grads,...  14.4 us
  transfers between devices with their start and end apart: 57, of which 33 were waited for; matrix products, arithmetic and copies ran while one was open for 3% of the time, Pallas kernels for 0%

profile of v2, /device:TPU:0, one launch (start us, length us, event | category | flops | bytes accessed | tf_op | source)
XLA Modules:
  0.0 156.5 jit_solution(4803712518873501173)
XLA Ops:
  3.0 3.1 %collective-permute-start.3 = (bf16[224,768]{1,0:T(8,128)(2,1)S(1)}, bf16[224,768]{1,0:T(8,128)(2,1)}, u32[]{:S(2)}, u32[]{:S(2)}) collective-permute-start(bf16[224,768]{1,0:T(8,128)(2,1)S(1)} %pad_maximum_fusion), channel_id=1, source_target_pairs={{0,8},{8,16},{16,24},{24,0},{1,9},{9,17},{17,25},{25,1},{2,10},{10... | collective-permute-start | bytes 1032200 | tf_op jit(solution)/shard_map/ppermute | solution.py:35
  6.1 2.1 %collective-permute-start.23 = (bf16[224,768]{1,0:T(8,128)(2,1)S(1)}, bf16[224,768]{1,0:T(8,128)(2,1)}, u32[]{:S(2)}, u32[]{:S(2)}) collective-permute-start(bf16[224,768]{1,0:T(8,128)(2,1)S(1)} %pad_maximum_fusion), channel_id=1, source_target_pairs={{0,24},{8,0},{16,8},{24,16},{1,25},{9,1},{17,9},{25,17},{2,26},{10... | collective-permute-start | bytes 1032200 | tf_op jit(solution)/shard_map/ppermute | solution.py:35
  9.8 7.4 %collective-permute-done.3.refs_16_ = bf16[224,768]{1,0:T(8,128)(2,1)} collective-permute-done((bf16[224,768]{1,0:T(8,128)(2,1)S(1)}, bf16[224,768]{1,0:T(8,128)(2,1)}, u32[]{:S(2)}, u32[]{:S(2)}) %collective-permute-start.3) | collective-permute-done | bytes 344096 | tf_op jit(solution)/shard_map/ppermute | solution.py:35
  17.2 1.7 %collective-permute-start.4 = (bf16[224,768]{1,0:T(8,128)(2,1)}, bf16[224,768]{1,0:T(8,128)(2,1)S(1)}, u32[]{:S(2)}, u32[]{:S(2)}) collective-permute-start(bf16[224,768]{1,0:T(8,128)(2,1)} %collective-permute-done.3.refs_16_), channel_id=1, source_target_pairs={{0,2},{1,3},{2,0},{3,1},{4,6},{5,7},{6,4},{7,5},{8,10},{9,11},{10,... | collective-permute-start | bytes 1032200 | tf_op jit(solution)/shard_map/ppermute | solution.py:40
  20.9 2.2 %collective-permute-done.23.refs_26_ = bf16[224,768]{1,0:T(8,128)(2,1)} collective-permute-done((bf16[224,768]{1,0:T(8,128)(2,1)S(1)}, bf16[224,768]{1,0:T(8,128)(2,1)}, u32[]{:S(2)}, u32[]{:S(2)}) %collective-permute-start.23) | collective-permute-done | bytes 344096 | tf_op jit(solution)/shard_map/ppermute | solution.py:35
  24.6 10.3 %collective-permute-start = (bf16[1,768]{1,0:T(2,128)(2,1)S(1)}, bf16[1,768]{1,0:T(2,128)(2,1)S(1)}, u32[]{:S(2)}, u32[]{:S(2)}) collective-permute-start(bf16[1,768]{1,0:T(2,128)(2,1)S(1)} %get-tuple-element.37), channel_id=1, source_target_pairs={{0,8},{8,16},{16,24},{24,0},{1,9},{9,17},{17,25},{25,1},{2,10},{10... | collective-permute-start | bytes 4616 | tf_op jit(solution)/shard_map/ppermute | solution.py:35
  36.3 4.3 %collective-permute-start.1 = (bf16[1,768]{1,0:T(2,128)(2,1)S(1)}, bf16[1,768]{1,0:T(2,128)(2,1)S(1)}, u32[]{:S(2)}, u32[]{:S(2)}) collective-permute-start(bf16[1,768]{1,0:T(2,128)(2,1)S(1)} %get-tuple-element.36), channel_id=1, source_target_pairs={{0,16},{8,24},{16,0},{24,8},{1,17},{9,25},{17,1},{25,9},{2,18},{10... | collective-permute-start | bytes 4616 | tf_op jit(solution)/shard_map/ppermute | solution.py:35
  42.1 2.4 %collective-permute-start.2 = (bf16[1,768]{1,0:T(2,128)(2,1)S(1)}, bf16[1,768]{1,0:T(2,128)(2,1)S(1)}, u32[]{:S(2)}, u32[]{:S(2)}) collective-permute-start(bf16[1,768]{1,0:T(2,128)(2,1)S(1)} %get-tuple-element.35), channel_id=1, source_target_pairs={{0,24},{8,0},{16,8},{24,16},{1,25},{9,1},{17,9},{25,17},{2,26},{10... | collective-permute-start | bytes 4616 | tf_op jit(solution)/shard_map/ppermute | solution.py:35
  50.3 4.8 %collective-permute-done.27.refs_30_ = bf16[224,768]{1,0:T(8,128)(2,1)S(1)} collective-permute-done((bf16[224,768]{1,0:T(8,128)(2,1)}, bf16[224,768]{1,0:T(8,128)(2,1)S(1)}, u32[]{:S(2)}, u32[]{:S(2)}) %collective-permute-start.27) | collective-permute-done | bytes 344096 | tf_op jit(solution)/shard_map/ppermute | solution.py:40
  55.1 2.7 %collective-permute-start.5 = (f32[1,1152]{1,0:T(1,128)S(1)}, f32[1,1152]{1,0:T(1,128)S(1)}, u32[]{:S(2)}, u32[]{:S(2)}) collective-permute-start(f32[1,1152]{1,0:T(1,128)S(1)} %get-tuple-element.32), channel_id=1, source_target_pairs={{0,24},{8,0},{16,8},{24,16},{1,25},{9,1},{17,9},{25,17},{2,26},{10... | collective-permute-start | bytes 13832 | tf_op jit(solution)/shard_map/ppermute | solution.py:35
  66.4 5.9 %collective-permute-done.9.refs_10_ = f32[1,1152]{1,0:T(1,128)S(1)} collective-permute-done((f32[1,1152]{1,0:T(1,128)S(1)}, f32[1,1152]{1,0:T(1,128)S(1)}, u32[]{:S(2)}, u32[]{:S(2)}) %collective-permute-start.9) | collective-permute-done | bytes 4640 | tf_op jit(solution)/shard_map/ppermute | solution.py:40
  72.8 3.1 %collective-permute-done.11.refs_12_ = f32[1,1152]{1,0:T(1,128)S(1)} collective-permute-done((f32[1,1152]{1,0:T(1,128)S(1)}, f32[1,1152]{1,0:T(1,128)S(1)}, u32[]{:S(2)}, u32[]{:S(2)}) %collective-permute-start.11) | collective-permute-done | bytes 4640 | tf_op jit(solution)/shard_map/ppermute | solution.py:40
  77.3 3.1 %collective-permute-done.13.refs_14_ = f32[1,1152]{1,0:T(1,128)S(1)} collective-permute-done((f32[1,1152]{1,0:T(1,128)S(1)}, f32[1,1152]{1,0:T(1,128)S(1)}, u32[]{:S(2)}, u32[]{:S(2)}) %collective-permute-start.13) | collective-permute-done | bytes 4640 | tf_op jit(solution)/shard_map/ppermute | solution.py:40
  87.8 3.8 %collective-permute-done.39.refs_42_ = bf16[112,768]{1,0:T(8,128)(2,1)S(1)} collective-permute-done((bf16[112,768]{1,0:T(8,128)(2,1)S(1)}, bf16[112,768]{1,0:T(8,128)(2,1)S(1)}, u32[]{:S(2)}, u32[]{:S(2)}) %collective-permute-start.39) | collective-permute-done | bytes 172064 | tf_op jit(solution)/shard_map/ppermute | solution.py:40
  97.5 14.4 %step.1 = (bf16[4,32,2048]{2,1,0:T(8,128)(2,1)}, bf16[4,32,2048]{2,1,0:T(8,128)(2,1)}, f32[128,3072]{1,0:T(8,128)}, f32[128,1536]{1,0:T(8,128)}) custom-call(bf16[128,1536]{1,0:T(8,128)(2,1)} %bitcast.59, bf16[128,1536]{1,0:T(8,128)(2,1)} %bitcast.60, bf16[128,3072]{1,0:T(8,128)(2,1)} %bitcast.56, bf16[128,3072]{1,0:T(8,128)(2,1)} %bitcast.57, ...), custom_call_target="tpu_custom_call" | custom-call | tf_op jit(solution)/shard_map/step/pallas_call | solution.py:302
  112.1 2.0 %collective-permute-done.43 = bf16[4,32,2048]{2,1,0:T(8,128)(2,1)S(1)} collective-permute-done((bf16[4,32,2048]{2,1,0:T(8,128)(2,1)}, bf16[4,32,2048]{2,1,0:T(8,128)(2,1)S(1)}, u32[]{:S(2)}, u32[]{:S(2)}) %collective-permute-start.43) | collective-permute-done | bytes 524320 | tf_op jit(solution)/shard_map/ppermute | solution.py:40
  118.9 2.5 %collective-permute-done.44 = bf16[4,8,2048]{2,1,0:T(8,128)(2,1)S(1)} collective-permute-done((bf16[4,8,2048]{2,1,0:T(8,128)(2,1)S(1)}, bf16[4,8,2048]{2,1,0:T(8,128)(2,1)S(1)}, u32[]{:S(2)}, u32[]{:S(2)}) %collective-permute-start.44) | collective-permute-done | bytes 131104 | tf_op jit(solution)/shard_map/ppermute | solution.py:40
  121.4 3.6 %collective-permute-done.45 = bf16[4,8,2048]{2,1,0:T(8,128)(2,1)S(1)} collective-permute-done((bf16[4,8,2048]{2,1,0:T(8,128)(2,1)S(1)}, bf16[4,8,2048]{2,1,0:T(8,128)(2,1)S(1)}, u32[]{:S(2)}, u32[]{:S(2)}) %collective-permute-start.45) | collective-permute-done | bytes 131104 | tf_op jit(solution)/shard_map/ppermute | solution.py:40
  126.4 2.1 %collective-permute-start.47 = (bf16[8,1920]{1,0:T(8,128)(2,1)S(1)}, bf16[8,1920]{1,0:T(8,128)(2,1)S(1)}, u32[]{:S(2)}, u32[]{:S(2)}) collective-permute-start(bf16[8,1920]{1,0:T(8,128)(2,1)S(1)} %get-tuple-element.29), channel_id=1, source_target_pairs={{0,8},{8,16},{16,24},{24,0},{1,9},{9,17},{17,25},{25,1},{2,10},{10... | collective-permute-start | bytes 92168 | tf_op jit(solution)/shard_map/ppermute | solution.py:35
  129.4 1.8 %collective-permute-start.49 = (bf16[8,1920]{1,0:T(8,128)(2,1)S(1)}, bf16[8,1920]{1,0:T(8,128)(2,1)S(1)}, u32[]{:S(2)}, u32[]{:S(2)}) collective-permute-start(bf16[8,1920]{1,0:T(8,128)(2,1)S(1)} %get-tuple-element.30), channel_id=1, source_target_pairs={{0,24},{8,0},{16,8},{24,16},{1,25},{9,1},{17,9},{25,17},{2,26},{10... | collective-permute-start | bytes 92168 | tf_op jit(solution)/shard_map/ppermute | solution.py:35
  138.6 1.7 %collective-permute-done.52 = bf16[8,1920]{1,0:T(8,128)(2,1)S(1)} collective-permute-done((bf16[8,1920]{1,0:T(8,128)(2,1)S(1)}, bf16[8,1920]{1,0:T(8,128)(2,1)S(1)}, u32[]{:S(2)}, u32[]{:S(2)}) %collective-permute-start.52) | collective-permute-done | bytes 30752 | tf_op jit(solution)/shard_map/ppermute | solution.py:40
  140.4 2.5 %multiply_convert_fusion = bf16[128,3072]{1,0:T(8,128)(2,1)} fusion(f32[128,3072]{1,0:T(8,128)} %get-tuple-element.20, f32[]{:T(128)S(6)} %div.30), kind=kLoop, calls=%fused_computation | loop fusion | flops 786432 | bytes 2359300 | tf_op jit(solution)/shard_map/convert_element_type | solution.py:585
  145.7 2.7 %collective-permute-start.55 = (f32[8,128]{1,0:T(8,128)S(1)}, f32[8,128]{1,0:T(8,128)S(1)}, u32[]{:S(2)}, u32[]{:S(2)}) collective-permute-start(f32[8,128]{1,0:T(8,128)S(1)} %broadcast_in_dim.2), channel_id=1, source_target_pairs={{0,16},{8,24},{16,0},{24,8},{1,17},{9,25},{17,1},{25,9},{2,18},{10... | collective-permute-start | bytes 12296 | tf_op jit(solution)/shard_map/ppermute | solution.py:35
  150.2 1.8 %collective-permute-done.56 = f32[8,128]{1,0:T(8,128)S(1)} collective-permute-done((f32[8,128]{1,0:T(8,128)S(1)}, f32[8,128]{1,0:T(8,128)S(1)}, u32[]{:S(2)}, u32[]{:S(2)}) %collective-permute-start.56) | collective-permute-done | bytes 4128 | tf_op jit(solution)/shard_map/ppermute | solution.py:35
  (219 shorter events, 60.0 us)
Async XLA Ops:
  3.0 14.2 %collective-permute-start.3 = (bf16[224,768]{1,0:T(8,128)(2,1)S(1)}, bf16[224,768]{1,0:T(8,128)(2,1)}, u32[]{:S(2)}, u32[]{:S(2)}) collective-permute-start(bf16[224,768]{1,0:T(8,128)(2,1)S(1)} %pad_maximum_fusion), channel_id=1, source_target_pairs={{0,8},{8,16},{16,24},{24,0},{1,9},{9,17},{17,25},{25,1},{2,10},{10... | collective-permute-start | bytes 1032200 | tf_op jit(solution)/shard_map/ppermute | solution.py:35
  6.1 17.0 %collective-permute-start.23 = (bf16[224,768]{1,0:T(8,128)(2,1)S(1)}, bf16[224,768]{1,0:T(8,128)(2,1)}, u32[]{:S(2)}, u32[]{:S(2)}) collective-permute-start(bf16[224,768]{1,0:T(8,128)(2,1)S(1)} %pad_maximum_fusion), channel_id=1, source_target_pairs={{0,24},{8,0},{16,8},{24,16},{1,25},{9,1},{17,9},{25,17},{2,26},{10... | collective-permute-start | bytes 1032200 | tf_op jit(solution)/shard_map/ppermute | solution.py:35
  8.2 38.4 %collective-permute-start.33 = (bf16[224,768]{1,0:T(8,128)(2,1)S(1)}, bf16[224,768]{1,0:T(8,128)(2,1)}, u32[]{:S(2)}, u32[]{:S(2)}) collective-permute-start(bf16[224,768]{1,0:T(8,128)(2,1)S(1)} %pad_maximum_fusion), channel_id=1, source_target_pairs={{0,16},{8,24},{16,0},{24,8},{1,17},{9,25},{17,1},{25,9},{2,18},{10... | collective-permute-start | bytes 1032200 | tf_op jit(solution)/shard_map/ppermute | solution.py:35
  17.2 30.9 %collective-permute-start.4 = (bf16[224,768]{1,0:T(8,128)(2,1)}, bf16[224,768]{1,0:T(8,128)(2,1)S(1)}, u32[]{:S(2)}, u32[]{:S(2)}) collective-permute-start(bf16[224,768]{1,0:T(8,128)(2,1)} %collective-permute-done.3.refs_16_), channel_id=1, source_target_pairs={{0,2},{1,3},{2,0},{3,1},{4,6},{5,7},{6,4},{7,5},{8,10},{9,11},{10,... | collective-permute-start | bytes 1032200 | tf_op jit(solution)/shard_map/ppermute | solution.py:40
  19.3 30.5 %collective-permute-start.17 = (bf16[224,768]{1,0:T(8,128)(2,1)}, bf16[224,768]{1,0:T(8,128)(2,1)S(1)}, u32[]{:S(2)}, u32[]{:S(2)}) collective-permute-start(bf16[224,768]{1,0:T(8,128)(2,1)} %collective-permute-done.3.refs_16_), channel_id=1, source_target_pairs={{0,4},{1,5},{2,6},{3,7},{4,0},{5,1},{6,2},{7,3},{8,12},{9,13},{10,... | collective-permute-start | bytes 1032200 | tf_op jit(solution)/shard_map/ppermute | solution.py:40
  23.1 26.7 %collective-permute-start.25 = (bf16[224,768]{1,0:T(8,128)(2,1)}, bf16[224,768]{1,0:T(8,128)(2,1)S(1)}, u32[]{:S(2)}, u32[]{:S(2)}) collective-permute-start(bf16[224,768]{1,0:T(8,128)(2,1)} %collective-permute-done.23.refs_26_), channel_id=1, source_target_pairs={{0,2},{1,3},{2,0},{3,1},{4,6},{5,7},{6,4},{7,5},{8,10},{9,11},{10,... | collective-permute-start | bytes 1032200 | tf_op jit(solution)/shard_map/ppermute | solution.py:40
  24.6 11.6 %collective-permute-start = (bf16[1,768]{1,0:T(2,128)(2,1)S(1)}, bf16[1,768]{1,0:T(2,128)(2,1)S(1)}, u32[]{:S(2)}, u32[]{:S(2)}) collective-permute-start(bf16[1,768]{1,0:T(2,128)(2,1)S(1)} %get-tuple-element.37), channel_id=1, source_target_pairs={{0,8},{8,16},{16,24},{24,0},{1,9},{9,17},{17,25},{25,1},{2,10},{10... | collective-permute-start | bytes 4616 | tf_op jit(solution)/shard_map/ppermute | solution.py:35
  45.9 9.2 %collective-permute-start.27 = (bf16[224,768]{1,0:T(8,128)(2,1)}, bf16[224,768]{1,0:T(8,128)(2,1)S(1)}, u32[]{:S(2)}, u32[]{:S(2)}) collective-permute-start(bf16[224,768]{1,0:T(8,128)(2,1)} %collective-permute-done.23.refs_26_), channel_id=1, source_target_pairs={{0,4},{1,5},{2,6},{3,7},{4,0},{5,1},{6,2},{7,3},{8,12},{9,13},{10,... | collective-permute-start | bytes 1032200 | tf_op jit(solution)/shard_map/ppermute | solution.py:40
  46.6 11.2 %collective-permute-start.35 = (bf16[224,768]{1,0:T(8,128)(2,1)}, bf16[224,768]{1,0:T(8,128)(2,1)S(1)}, u32[]{:S(2)}, u32[]{:S(2)}) collective-permute-start(bf16[224,768]{1,0:T(8,128)(2,1)} %collective-permute-done.33.refs_36_), channel_id=1, source_target_pairs={{0,2},{1,3},{2,0},{3,1},{4,6},{5,7},{6,4},{7,5},{8,10},{9,11},{10,... | collective-permute-start | bytes 1032200 | tf_op jit(solution)/shard_map/ppermute | solution.py:40
  48.1 10.7 %collective-permute-start.37 = (bf16[224,768]{1,0:T(8,128)(2,1)}, bf16[224,768]{1,0:T(8,128)(2,1)S(1)}, u32[]{:S(2)}, u32[]{:S(2)}) collective-permute-start(bf16[224,768]{1,0:T(8,128)(2,1)} %collective-permute-done.33.refs_36_), channel_id=1, source_target_pairs={{0,4},{1,5},{2,6},{3,7},{4,0},{5,1},{6,2},{7,3},{8,12},{9,13},{10,... | collective-permute-start | bytes 1032200 | tf_op jit(solution)/shard_map/ppermute | solution.py:40
  49.7 10.6 %collective-permute-start.15 = (bf16[224,768]{1,0:T(8,128)(2,1)}, bf16[224,768]{1,0:T(8,128)(2,1)S(1)}, u32[]{:S(2)}, u32[]{:S(2)}) collective-permute-start(bf16[224,768]{1,0:T(8,128)(2,1)} %collective-permute-done.3.refs_16_), channel_id=1, source_target_pairs={{0,1},{1,0},{2,3},{3,2},{4,5},{5,4},{6,7},{7,6},{8,9},{9,8},{10,11... | collective-permute-start | bytes 1032200 | tf_op jit(solution)/shard_map/ppermute | solution.py:40
  49.8 10.6 %collective-permute-start.24 = (bf16[224,768]{1,0:T(8,128)(2,1)}, bf16[224,768]{1,0:T(8,128)(2,1)S(1)}, u32[]{:S(2)}, u32[]{:S(2)}) collective-permute-start(bf16[224,768]{1,0:T(8,128)(2,1)} %collective-permute-done.23.refs_26_), channel_id=1, source_target_pairs={{0,1},{1,0},{2,3},{3,2},{4,5},{5,4},{6,7},{7,6},{8,9},{9,8},{10,11... | collective-permute-start | bytes 1032200 | tf_op jit(solution)/shard_map/ppermute | solution.py:40
  55.1 6.9 %collective-permute-start.5 = (f32[1,1152]{1,0:T(1,128)S(1)}, f32[1,1152]{1,0:T(1,128)S(1)}, u32[]{:S(2)}, u32[]{:S(2)}) collective-permute-start(f32[1,1152]{1,0:T(1,128)S(1)} %get-tuple-element.32), channel_id=1, source_target_pairs={{0,24},{8,0},{16,8},{24,16},{1,25},{9,1},{17,9},{25,17},{2,26},{10... | collective-permute-start | bytes 13832 | tf_op jit(solution)/shard_map/ppermute | solution.py:35
  60.5 25.1 %collective-permute-start.19 = (bf16[112,768]{1,0:T(8,128)(2,1)S(1)}, bf16[112,768]{1,0:T(8,128)(2,1)S(1)}, u32[]{:S(2)}, u32[]{:S(2)}) collective-permute-start(bf16[112,768]{1,0:T(8,128)(2,1)S(1)} %slice.84), channel_id=1, source_target_pairs={{0,4},{1,5},{2,6},{3,7},{4,0},{5,1},{6,2},{7,3},{8,12},{9,13},{10,... | collective-permute-start | bytes 516104 | tf_op jit(solution)/shard_map/ppermute | solution.py:40
  62.1 25.0 %collective-permute-start.21 = (bf16[112,768]{1,0:T(8,128)(2,1)S(1)}, bf16[112,768]{1,0:T(8,128)(2,1)S(1)}, u32[]{:S(2)}, u32[]{:S(2)}) collective-permute-start(bf16[112,768]{1,0:T(8,128)(2,1)S(1)} %slice.85), channel_id=1, source_target_pairs={{0,2},{1,3},{2,0},{3,1},{4,6},{5,7},{6,4},{7,5},{8,10},{9,11},{10,... | collective-permute-start | bytes 516104 | tf_op jit(solution)/shard_map/ppermute | solution.py:40
  63.6 23.5 %collective-permute-start.29 = (bf16[112,768]{1,0:T(8,128)(2,1)S(1)}, bf16[112,768]{1,0:T(8,128)(2,1)S(1)}, u32[]{:S(2)}, u32[]{:S(2)}) collective-permute-start(bf16[112,768]{1,0:T(8,128)(2,1)S(1)} %slice.86), channel_id=1, source_target_pairs={{0,4},{1,5},{2,6},{3,7},{4,0},{5,1},{6,2},{7,3},{8,12},{9,13},{10,... | collective-permute-start | bytes 516104 | tf_op jit(solution)/shard_map/ppermute | solution.py:40
  64.2 23.4 %collective-permute-start.31 = (bf16[112,768]{1,0:T(8,128)(2,1)S(1)}, bf16[112,768]{1,0:T(8,128)(2,1)S(1)}, u32[]{:S(2)}, u32[]{:S(2)}) collective-permute-start(bf16[112,768]{1,0:T(8,128)(2,1)S(1)} %slice.87), channel_id=1, source_target_pairs={{0,2},{1,3},{2,0},{3,1},{4,6},{5,7},{6,4},{7,5},{8,10},{9,11},{10,... | collective-permute-start | bytes 516104 | tf_op jit(solution)/shard_map/ppermute | solution.py:40
  65.8 6.5 %collective-permute-start.9 = (f32[1,1152]{1,0:T(1,128)S(1)}, f32[1,1152]{1,0:T(1,128)S(1)}, u32[]{:S(2)}, u32[]{:S(2)}) collective-permute-start(f32[1,1152]{1,0:T(1,128)S(1)} %fusion.19.refs_8_), channel_id=1, source_target_pairs={{0,2},{1,3},{2,0},{3,1},{4,6},{5,7},{6,4},{7,5},{8,10},{9,11},{10,... | collective-permute-start | bytes 13832 | tf_op jit(solution)/shard_map/ppermute | solution.py:40
  85.1 6.4 %collective-permute-start.39 = (bf16[112,768]{1,0:T(8,128)(2,1)S(1)}, bf16[112,768]{1,0:T(8,128)(2,1)S(1)}, u32[]{:S(2)}, u32[]{:S(2)}) collective-permute-start(bf16[112,768]{1,0:T(8,128)(2,1)S(1)} %slice.88), channel_id=1, source_target_pairs={{0,4},{1,5},{2,6},{3,7},{4,0},{5,1},{6,2},{7,3},{8,12},{9,13},{10,... | collective-permute-start | bytes 516104 | tf_op jit(solution)/shard_map/ppermute | solution.py:40
  85.6 6.2 %collective-permute-start.41 = (bf16[112,768]{1,0:T(8,128)(2,1)S(1)}, bf16[112,768]{1,0:T(8,128)(2,1)S(1)}, u32[]{:S(2)}, u32[]{:S(2)}) collective-permute-start(bf16[112,768]{1,0:T(8,128)(2,1)S(1)} %slice.89), channel_id=1, source_target_pairs={{0,2},{1,3},{2,0},{3,1},{4,6},{5,7},{6,4},{7,5},{8,10},{9,11},{10,... | collective-permute-start | bytes 516104 | tf_op jit(solution)/shard_map/ppermute | solution.py:40
  87.6 6.8 %collective-permute-start.16 = (bf16[224,768]{1,0:T(8,128)(2,1)S(1)}, bf16[224,768]{1,0:T(8,128)(2,1)S(1)}, u32[]{:S(2)}, u32[]{:S(2)}) collective-permute-start(bf16[224,768]{1,0:T(8,128)(2,1)S(1)} %collective-permute-done.4.refs_18_), channel_id=1, source_target_pairs={{0,1},{1,0},{2,3},{3,2},{4,5},{5,4},{6,7},{7,6},{8,9},{9,8},{10,11... | collective-permute-start | bytes 1032200 | tf_op jit(solution)/shard_map/ppermute | solution.py:40
  115.3 6.0 %collective-permute-start.44 = (bf16[4,8,2048]{2,1,0:T(8,128)(2,1)S(1)}, bf16[4,8,2048]{2,1,0:T(8,128)(2,1)S(1)}, u32[]{:S(2)}, u32[]{:S(2)}) collective-permute-start(bf16[4,8,2048]{2,1,0:T(8,128)(2,1)S(1)} %get-tuple-element.24), channel_id=1, source_target_pairs={{0,2},{1,3},{2,0},{3,1},{4,6},{5,7},{6,4},{7,5},{8,10},{9,11},{10,... | collective-permute-start | bytes 393224 | tf_op jit(solution)/shard_map/ppermute | solution.py:40
  116.9 8.1 %collective-permute-start.45 = (bf16[4,8,2048]{2,1,0:T(8,128)(2,1)S(1)}, bf16[4,8,2048]{2,1,0:T(8,128)(2,1)S(1)}, u32[]{:S(2)}, u32[]{:S(2)}) collective-permute-start(bf16[4,8,2048]{2,1,0:T(8,128)(2,1)S(1)} %get-tuple-element.26), channel_id=1, source_target_pairs={{0,4},{1,5},{2,6},{3,7},{4,0},{5,1},{6,2},{7,3},{8,12},{9,13},{10,... | collective-permute-start | bytes 393224 | tf_op jit(solution)/shard_map/ppermute | solution.py:40
  118.0 7.0 %collective-permute-start.46 = (bf16[4,8,2048]{2,1,0:T(8,128)(2,1)S(1)}, bf16[4,8,2048]{2,1,0:T(8,128)(2,1)S(1)}, u32[]{:S(2)}, u32[]{:S(2)}) collective-permute-start(bf16[4,8,2048]{2,1,0:T(8,128)(2,1)S(1)} %get-tuple-element.25), channel_id=1, source_target_pairs={{0,6},{1,7},{2,4},{3,5},{4,2},{5,3},{6,0},{7,1},{8,14},{9,15},{10,... | collective-permute-start | bytes 393224 | tf_op jit(solution)/shard_map/ppermute | solution.py:40
  (72 other events, 803.2 us)
